TPU v7x, 32 devices: a whole 2x2x4 slice. The times are simulated.
32 devices in a mesh: row: 4 (over y, x), col: 4 (over z), band: 2 (over core).
Axes of the slice: x: 2, y: 2, z: 4, core: 2. Of those that a mesh axis runs over, the one named last changes fastest.
Arguments:
- freq_index: int32 [2], replicated, may hold values from 0 to 32
- band_energy: float32 [8], replicated, may hold values from -4 to 4
- pole_amp: float32 [4096, 4096], P('row', 'col'), may hold values from -6 to 6
- pole_freq: float32 [4096, 4096], P('row', 'col'), may hold values from 0.5 to 4
- left_pieces: bfloat16 [8, 256, 4096], P(('col', 'band'), None, 'row'), may hold values from -0.055664062 to 0.055664062
- right_pieces: bfloat16 [8, 256, 4096], P(('row', 'band'), None, 'col'), may hold values from -0.055664062 to 0.055664062
Outputs:
- sigma: float32 [2, 256, 256], P(None, ('row', 'col', 'band'))
All inputs are finite; a program needn't handle non-finite values.
Results may differ from a plain program's by a relative error of at most 0.0055.
Values may be sent and summed in bfloat16 or wider, within the bound.
No kernel may reach another device: no remote copies, remote signals or barrier semaphores. Data moves between devices by JAX's collectives and lax.ppermute only.
A program may use at most 128 MiB of HBM per device.

v0:
```python
import jax
import jax.numpy as jnp
from jax import lax
from jax.sharding import PartitionSpec as P


def body(freq_index, band_energy, pole_amp, pole_freq, left_pieces, right_pieces):
    bpiece = left_pieces.shape[0]
    nstate = left_pieces.shape[1]
    nfreq = freq_index.shape[0]
    nband = lax.axis_size("band")
    group = lax.axis_index("band")
    freq = -4.0 + 0.25 * freq_index.astype(jnp.float32)
    right_all = lax.all_gather(right_pieces, "row", axis=0, tiled=True)

    def energy_at(position):
        overall = (position // bpiece * nband + group) * bpiece + position % bpiece
        return lax.dynamic_index_in_dim(band_energy, overall, 0, False)

    def add_band(total, left_band, position):
        right_band = lax.dynamic_index_in_dim(right_all, position, 0, False)
        energy = energy_at(position)
        results = []
        for w in range(nfreq):
            distance = freq[w] - energy - pole_freq
            screened = (pole_amp * distance / (distance * distance + 0.25)).astype(jnp.bfloat16)
            partial_value = jnp.dot(left_band, screened, preferred_element_type=jnp.float32).astype(
                jnp.bfloat16
            )
            results.append(
                lax.dot_general(
                    partial_value,
                    right_band,
                    (((1,), (1,)), ((), ())),
                    preferred_element_type=jnp.float32,
                )
            )
        return total + jnp.stack(results)

    start = jnp.zeros((nfreq, nstate, nstate), jnp.float32)
    left_all = lax.all_gather(left_pieces, "col", axis=0, tiled=True)

    def step(index, carry):
        left_band = lax.dynamic_index_in_dim(left_all, index, 0, False)
        return add_band(carry, left_band, index)

    total = lax.fori_loop(0, left_all.shape[0], step, start)
    summed = lax.psum(total, ("row", "col", "band"))
    owned = nstate // lax.axis_size(("row", "col", "band"))
    sigma = lax.dynamic_slice_in_dim(
        summed, lax.axis_index(("row", "col", "band")) * owned, owned, 1
    )
    return sigma


def solution(mesh):
    in_specs = (
        P(),
        P(),
        P("row", "col"),
        P("row", "col"),
        P(("col", "band"), None, "row"),
        P(("row", "band"), None, "col"),
    )
    out_specs = P(None, ("row", "col", "band"), None)
    return jax.shard_map(body, mesh=mesh, in_specs=in_specs, out_specs=out_specs, check_vma=False)
```

profile of v0, /device:TPU:0, one launch (start us, length us, event | category | flops | bytes accessed | tf_op | source)
XLA Modules:
  0.0 290.5 jit_solution(17561359348349133035)
XLA Ops:
  6.5 0.7 all-gather.3.cloned.1.call-update
  7.3 0.0 all-gather.5.cloned.1.call-start
  7.3 0.7 all-gather.5.cloned.1.call-update
  8.0 0.0 all-reduce.2.cloned.1.call-start
  8.1 0.7 multiply_add_fusion
  8.7 48.6 %all-gather.3.cloned.1.call-done = bf16[4,256,1024]{2,1,0:T(8,128)(2,1)} async-done(((bf16[1,256,1024]{2,1,0:T(8,128)(2,1)}), bf16[4,256,1024]{2,1,0:T(8,128)(2,1)}) %all-gather.3.cloned.1.call-update) | async-done | bytes 2097168 | tf_op jit(solution)/shard_map/all_gather | solution.py:41
  57.3 35.9 %all-gather.5.cloned.1.call-done = bf16[4,256,1024]{2,1,0:T(8,128)(2,1)} async-done(((bf16[1,256,1024]{2,1,0:T(8,128)(2,1)}), bf16[4,256,1024]{2,1,0:T(8,128)(2,1)}) %all-gather.5.cloned.1.call-update) | async-done | bytes 2097168 | tf_op jit(solution)/shard_map/all_gather | solution.py:14
  93.2 59.5 %while.17 = (s32[]{:T(128)}, f32[2,256,256]{2,1,0:T(8,128)S(1)}, bf16[4,256,1024]{2,1,0:T(8,128)(2,1)}, f32[2]{0:T(128)S(1)}, s32[]{:T(128)}, /*index=5*/f32[8]{...) while((s32[]{:T(128)}, f32[2,256,256]{2,1,0:T(8,128)S(1)}, ...), condition=%wide.region_1.2_spmd.clone, body=%wide.region_0.1_spmd.clone.sunk | while | flops 1355677696 | bytes 20974844 | solution.py:47
  93.2 1.3 dynamic_slice.70
  94.5 0.6 fusion.34
  97.7 5.1 %convolution_bitcast_fusion.4 = f32[1,256,256]{2,1,0:T(8,128)S(1)} fusion(f32[1024,1024]{1,0:T(8,128)} %get-tuple-element.398, f32[1024,1024]{1,0:T(8,128)} %get-tuple-element.397, f32[]{:T(128)} %bitcast.32, bf16[4,256,1024]{2,1,0:T(8,128)(2,1)} %get-tuple-element.399, s32[]{:T(128)S(6)} %copy.9, bf16[4,256,1024]{2,1,0:T(8,128)(2,1)} %get-tuple-element.393), kind=kOutput, calls=%fused_computation.6.clone.1 | convolution fusion | flops 677642240 | bytes 9700864 | tf_op jit(solution)/shard_map/while/body/eval_jaxpr/dot_general | solution.py:31
  102.8 5.1 %convolution_bitcast_fusion.5 = f32[1,256,256]{2,1,0:T(8,128)S(1)} fusion(f32[1024,1024]{1,0:T(8,128)} %get-tuple-element.398, f32[1024,1024]{1,0:T(8,128)} %get-tuple-element.397, f32[]{:T(128)} %bitcast.33, bf16[4,256,1024]{2,1,0:T(8,128)(2,1)} %get-tuple-element.399, s32[]{:T(128)S(6)} %copy.9, bf16[4,256,1024]{2,1,0:T(8,128)(2,1)} %get-tuple-element.393), kind=kOutput, calls=%fused_computation.7.clone.1 | convolution fusion | flops 677642240 | bytes 9700864 | tf_op jit(solution)/shard_map/while/body/eval_jaxpr/dot_general | solution.py:31
  107.9 0.1 maximum_add_fusion.2
  108.0 1.3 dynamic_slice.70
  109.4 0.6 fusion.34
  112.6 5.1 %convolution_bitcast_fusion.4 = f32[1,256,256]{2,1,0:T(8,128)S(1)} fusion(f32[1024,1024]{1,0:T(8,128)} %get-tuple-element.398, f32[1024,1024]{1,0:T(8,128)} %get-tuple-element.397, f32[]{:T(128)} %bitcast.32, bf16[4,256,1024]{2,1,0:T(8,128)(2,1)} %get-tuple-element.399, s32[]{:T(128)S(6)} %copy.9, bf16[4,256,1024]{2,1,0:T(8,128)(2,1)} %get-tuple-element.393), kind=kOutput, calls=%fused_computation.6.clone.1 | convolution fusion | flops 677642240 | bytes 9700864 | tf_op jit(solution)/shard_map/while/body/eval_jaxpr/dot_general | solution.py:31
  117.7 5.1 %convolution_bitcast_fusion.5 = f32[1,256,256]{2,1,0:T(8,128)S(1)} fusion(f32[1024,1024]{1,0:T(8,128)} %get-tuple-element.398, f32[1024,1024]{1,0:T(8,128)} %get-tuple-element.397, f32[]{:T(128)} %bitcast.33, bf16[4,256,1024]{2,1,0:T(8,128)(2,1)} %get-tuple-element.399, s32[]{:T(128)S(6)} %copy.9, bf16[4,256,1024]{2,1,0:T(8,128)(2,1)} %get-tuple-element.393), kind=kOutput, calls=%fused_computation.7.clone.1 | convolution fusion | flops 677642240 | bytes 9700864 | tf_op jit(solution)/shard_map/while/body/eval_jaxpr/dot_general | solution.py:31
  122.7 0.1 maximum_add_fusion.2
  122.9 1.3 dynamic_slice.70
  124.2 0.6 fusion.34
  127.5 5.1 %convolution_bitcast_fusion.4 = f32[1,256,256]{2,1,0:T(8,128)S(1)} fusion(f32[1024,1024]{1,0:T(8,128)} %get-tuple-element.398, f32[1024,1024]{1,0:T(8,128)} %get-tuple-element.397, f32[]{:T(128)} %bitcast.32, bf16[4,256,1024]{2,1,0:T(8,128)(2,1)} %get-tuple-element.399, s32[]{:T(128)S(6)} %copy.9, bf16[4,256,1024]{2,1,0:T(8,128)(2,1)} %get-tuple-element.393), kind=kOutput, calls=%fused_computation.6.clone.1 | convolution fusion | flops 677642240 | bytes 9700864 | tf_op jit(solution)/shard_map/while/body/eval_jaxpr/dot_general | solution.py:31
  132.5 5.1 %convolution_bitcast_fusion.5 = f32[1,256,256]{2,1,0:T(8,128)S(1)} fusion(f32[1024,1024]{1,0:T(8,128)} %get-tuple-element.398, f32[1024,1024]{1,0:T(8,128)} %get-tuple-element.397, f32[]{:T(128)} %bitcast.33, bf16[4,256,1024]{2,1,0:T(8,128)(2,1)} %get-tuple-element.399, s32[]{:T(128)S(6)} %copy.9, bf16[4,256,1024]{2,1,0:T(8,128)(2,1)} %get-tuple-element.393), kind=kOutput, calls=%fused_computation.7.clone.1 | convolution fusion | flops 677642240 | bytes 9700864 | tf_op jit(solution)/shard_map/while/body/eval_jaxpr/dot_general | solution.py:31
  137.6 0.1 maximum_add_fusion.2
  137.8 1.3 dynamic_slice.70
  139.1 0.6 fusion.34
  142.3 5.1 %convolution_bitcast_fusion.4 = f32[1,256,256]{2,1,0:T(8,128)S(1)} fusion(f32[1024,1024]{1,0:T(8,128)} %get-tuple-element.398, f32[1024,1024]{1,0:T(8,128)} %get-tuple-element.397, f32[]{:T(128)} %bitcast.32, bf16[4,256,1024]{2,1,0:T(8,128)(2,1)} %get-tuple-element.399, s32[]{:T(128)S(6)} %copy.9, bf16[4,256,1024]{2,1,0:T(8,128)(2,1)} %get-tuple-element.393), kind=kOutput, calls=%fused_computation.6.clone.1 | convolution fusion | flops 677642240 | bytes 9700864 | tf_op jit(solution)/shard_map/while/body/eval_jaxpr/dot_general | solution.py:31
  147.4 5.1 %convolution_bitcast_fusion.5 = f32[1,256,256]{2,1,0:T(8,128)S(1)} fusion(f32[1024,1024]{1,0:T(8,128)} %get-tuple-element.398, f32[1024,1024]{1,0:T(8,128)} %get-tuple-element.397, f32[]{:T(128)} %bitcast.33, bf16[4,256,1024]{2,1,0:T(8,128)(2,1)} %get-tuple-element.399, s32[]{:T(128)S(6)} %copy.9, bf16[4,256,1024]{2,1,0:T(8,128)(2,1)} %get-tuple-element.393), kind=kOutput, calls=%fused_computation.7.clone.1 | convolution fusion | flops 677642240 | bytes 9700864 | tf_op jit(solution)/shard_map/while/body/eval_jaxpr/dot_general | solution.py:31
  152.5 0.1 maximum_add_fusion.2
  152.6 0.8 copy-done
  153.4 0.0 all-reduce.2.cloned.1.call-update
  153.4 129.2 %all-reduce.2.cloned.1.call-done = f32[2,256,256]{2,1,0:T(8,128)} async-done(((f32[2,256,256]{2,1,0:T(8,128)}), f32[2,256,256]{2,1,0:T(8,128)}) %all-reduce.2.cloned.1.call-update) | async-done | bytes 524304 | tf_op jit(solution)/shard_map/psum | solution.py:48
  282.6 1.3 constant_dynamic-slice_fusion
  (3 shorter events, 0.0 us)
Async XLA Ops:
  6.5 50.8 %all-gather.3.cloned.1.call-start = ((), (), s32[]{:S(2)}) async-start(), calls=%async_computation | async-start | bytes 2621440 | tf_op jit(solution)/shard_map/all_gather | solution.py:41
  7.3 85.9 %all-gather.5.cloned.1.call-start = ((), (), s32[]{:S(2)}) async-start(), calls=%async_computation.1 | async-start | bytes 2621440 | tf_op jit(solution)/shard_map/all_gather | solution.py:14
  8.0 274.6 %all-reduce.2.cloned.1.call-start = ((), (), s32[]{:S(2)}) async-start(), calls=%async_computation.2 | async-start | bytes 1048576 | tf_op jit(solution)/shard_map/psum | solution.py:48
  152.6 0.8 copy-start
Sparse Core Ops, SparseCore 0:
  8.9 48.3 all-gather.2
  59.2 33.9 all-gather.4
  153.6 129.0 all-reduce.1
where the time goes:
time: 291 us; the launch traced here: 290 us
  waiting for transfers between devices  215 us (74%)
  matrix products  40.5 us (14%)
  between operations  13.1 us (5%)
  loops' own time  10.7 us (4%)
  local copies, waits for them, and re-layouts  9.74 us (3%)
    psum x1, waiting for transfers between devices, body(): summed = lax.psum(total, ('row', 'col', 'band'))  129 us
    all_gather x1, waiting for transfers between devices, body(): left_all = lax.all_gather(left_pieces, 'col', axis=0, tiled=True)  48.6 us
    dot_general x8, matrix products, add_band(): lax.dot_general(partial_value, right_band, (((1,), (1,)), ((), ())), pref...  40.5 us
    all_gather x1, waiting for transfers between devices, body(): right_all = lax.all_gather(right_pieces, 'row', axis=0, tiled=True)  35.9 us
    another operation x1, loops' own time, body(): total = lax.fori_loop(0, left_all.shape[0], step, start)  10.7 us
  transfers between devices with their start and end apart: 3, of which 3 were waited for; matrix products, arithmetic and copies ran while one was open for 0% of the time, Pallas kernels for 0%

commit v1 on v0

v1 whole, which is shorter than its diff:
```python
import functools

import jax
import jax.numpy as jnp
from jax import lax
from jax.experimental import pallas as pl
from jax.experimental.pallas import tpu as pltpu
from jax.sharding import PartitionSpec as P

ROWS = 128
SMALL = 16
COLUMNS = 256
VMEM_LIMIT = 12 * 1024 * 1024

WHOLE = pl.BlockSpec(memory_space=pltpu.VMEM)
SCALARS = pl.BlockSpec(memory_space=pltpu.SMEM)


def store_screened(xs, amp_ref, freq_ref, rows, columns, out_ref):
    nfreq = out_ref.shape[1]
    for at in range(0, amp_ref.shape[1], columns):
        here = slice(at, at + columns)
        amp, freq = amp_ref[rows, here], freq_ref[rows, here]
        for n, x in enumerate(xs):
            d = x - freq
            out_ref[n // nfreq, n % nfreq, rows, here] = (amp * d / (d * d + 0.25)).astype(
                jnp.bfloat16
            )


def times_right(s, right):
    return lax.dot_general(
        s, right, (((1,), (1,)), ((), ())), preferred_element_type=jnp.float32
    ).astype(jnp.bfloat16)


def shifts(arrivals, nband, bpiece, places, place_ref, index_ref, energy_ref):
    out = []
    for n in places:
        for k in range(bpiece):
            band = (arrivals(n, place_ref[0]) * nband + place_ref[2]) * bpiece + k
            for w in range(index_ref.shape[0]):
                out.append(-4.0 + 0.25 * index_ref[w].astype(jnp.float32) - energy_ref[band])
    return out


def screen_kernel(
    arrivals,
    nband,
    bpiece,
    place_ref,
    index_ref,
    energy_ref,
    amp_hbm,
    freq_hbm,
    ahead_ref,
    amp_ref,
    freq_ref,
    sems,
):
    steps = sems.shape[0]
    rows = amp_ref.shape[0] // steps

    def copies(i):
        here = pl.ds(pl.multiple_of(i * rows, rows), rows)
        return [
            pltpu.make_async_copy(src.at[here, :], dst.at[here, :], sems.at[i, k])
            for k, (src, dst) in enumerate(((amp_hbm, amp_ref), (freq_hbm, freq_ref)))
        ]

    for i in range(steps):
        for copy in copies(i):
            copy.start()
    xs = shifts(arrivals, nband, bpiece, (0, 1), place_ref, index_ref, energy_ref)

    @pl.loop(0, steps)
    def _(i):
        for copy in copies(i):
            copy.wait()

        @pl.loop(0, rows // SMALL)
        def _(j):
            here = pl.ds(pl.multiple_of(i * rows + j * SMALL, SMALL), SMALL)
            store_screened(xs, amp_ref, freq_ref, here, COLUMNS, ahead_ref)


def screen(place, arrivals, nband, bpiece, freq_index, band_energy, amp, freq):
    g, h = amp.shape
    nfreq = freq_index.shape[0]
    rows = min(ROWS, g)
    held = 8 * g * h + 4 * nfreq * g * bpiece * h
    return pl.pallas_call(
        functools.partial(screen_kernel, arrivals, nband, bpiece),
        in_specs=[SCALARS] * 3 + [pl.BlockSpec(memory_space=pl.ANY)] * 2,
        out_specs=[WHOLE] * 3,
        out_shape=[
            jax.ShapeDtypeStruct((2 * bpiece, nfreq, g, h), jnp.bfloat16),
            jax.ShapeDtypeStruct((g, h), jnp.float32),
            jax.ShapeDtypeStruct((g, h), jnp.float32),
        ],
        scratch_shapes=[pltpu.SemaphoreType.DMA((g // rows, 2))],
        cost_estimate=pl.CostEstimate(
            flops=1024 * bpiece * g * h * nfreq, bytes_accessed=8 * g * h, transcendentals=0
        ),
        compiler_params=pltpu.CompilerParams(vmem_limit_bytes=VMEM_LIMIT + held),
        name="screen",
    )(
        place,
        freq_index,
        band_energy,
        *(pltpu.with_memory_space_constraint(x, pltpu.HBM) for x in (amp, freq)),
    )


def more_kernel(
    arrivals, nband, bpiece, place_ref, index_ref, energy_ref, amp_ref, freq_ref, ahead_ref
):
    places = range(2, 2 + ahead_ref.shape[0] // bpiece)
    xs = shifts(arrivals, nband, bpiece, places, place_ref, index_ref, energy_ref)

    @pl.loop(0, amp_ref.shape[0] // SMALL)
    def _(i):
        here = pl.ds(pl.multiple_of(i * SMALL, SMALL), SMALL)
        store_screened(xs, amp_ref, freq_ref, here, COLUMNS, ahead_ref)


def screen_more(place, arrivals, nband, count, bpiece, freq_index, band_energy, amp, freq):
    g, h = amp.shape
    nfreq = freq_index.shape[0]
    held = 8 * g * h + 2 * nfreq * g * h * count * bpiece
    return pl.pallas_call(
        functools.partial(more_kernel, arrivals, nband, bpiece),
        in_specs=[SCALARS] * 3 + [WHOLE] * 2,
        out_specs=WHOLE,
        out_shape=jax.ShapeDtypeStruct((count * bpiece, nfreq, g, h), jnp.bfloat16),
        cost_estimate=pl.CostEstimate(
            flops=512 * count * bpiece * g * h * nfreq, bytes_accessed=8 * g * h, transcendentals=0
        ),
        compiler_params=pltpu.CompilerParams(vmem_limit_bytes=VMEM_LIMIT + held),
        name="more",
    )(place, freq_index, band_energy, amp, freq)


def apply_kernel(first, ahead_ref, *refs):
    rights, out_ref = refs[:-1], refs[-1]
    for k, right_ref in enumerate(rights):
        nstate = right_ref.shape[0]
        for w in range(ahead_ref.shape[1]):
            out_ref[k, :, w * nstate : (w + 1) * nstate] = times_right(
                ahead_ref[first + k, w], right_ref[...]
            )


def apply_rights(ahead, first, rights):
    count = len(rights)
    _, nfreq, g, h = ahead.shape
    nstate = rights[0].shape[0]
    return pl.pallas_call(
        functools.partial(apply_kernel, first),
        in_specs=[WHOLE] * (count + 1),
        out_specs=WHOLE,
        out_shape=jax.ShapeDtypeStruct((count, g, nfreq * nstate), jnp.bfloat16),
        cost_estimate=pl.CostEstimate(
            flops=2 * count * g * h * nfreq * nstate,
            bytes_accessed=2 * count * nfreq * g * h,
            transcendentals=0,
        ),
        compiler_params=pltpu.CompilerParams(vmem_limit_bytes=VMEM_LIMIT + 2 * ahead.size),
        name="apply",
    )(ahead, *rights)


def fold_kernel(slots, ntables, has_init, place_ref, *rest):
    count = len(slots)
    lefts = rest[:count]
    tables = rest[count : count + ntables]
    out_ref, acc = rest[-2], rest[-1]
    acc[...] = rest[-3][...] if has_init else jnp.zeros_like(acc)
    here = [place_ref[i] for i in range(3)]
    for left_ref, (slot_of, use_of, k) in zip(lefts, slots):
        slot = slot_of(*here)
        for at, table_ref in enumerate(tables):
            chosen = slot == at if use_of is None else (slot == at) & use_of(*here)

            @pl.when(chosen)
            def _():
                acc[...] += jnp.dot(
                    left_ref[...], table_ref[k], preferred_element_type=jnp.float32
                )

    out_ref[...] = acc[...].astype(out_ref.dtype)


def fold(place, pieces, tables, init, nstate, dtype):
    lefts, slots = zip(*pieces)
    g, width = tables[0].shape[1:]
    args = [place, *lefts, *tables]
    if init is not None:
        args.append(init)
    return pl.pallas_call(
        functools.partial(fold_kernel, slots, len(tables), init is not None),
        in_specs=[SCALARS] + [WHOLE] * (len(args) - 1),
        out_specs=WHOLE,
        scratch_shapes=[pltpu.VMEM((nstate, width), jnp.float32)],
        out_shape=jax.ShapeDtypeStruct((nstate, width), dtype),
        cost_estimate=pl.CostEstimate(
            flops=2 * len(lefts) * nstate * g * width,
            bytes_accessed=2 * len(lefts) * g * (width + nstate),
            transcendentals=0,
        ),
        compiler_params=pltpu.CompilerParams(vmem_limit_bytes=VMEM_LIMIT),
        name="fold",
    )(*args)


def xor_pairs(n, d):
    return [(i, i ^ d) for i in range(n)]


def gather_xor(piece, axis):
    n = lax.axis_size(axis)
    if n & (n - 1):
        me = lax.axis_index(axis)
        every = lax.all_gather(piece, axis, axis=0)
        return [
            lax.dynamic_index_in_dim(every, (me + d) % n, 0, False) for d in range(n)
        ], lambda d, me: (me + d) % n
    found = [piece] + [lax.ppermute(piece, axis, xor_pairs(n, d)) for d in range(1, n)]
    return found, lambda d, me: d ^ me


def is_line(ncol):
    return ncol == 4


def body(freq_index, band_energy, pole_amp, pole_freq, left_pieces, right_pieces):
    bpiece, nstate = left_pieces.shape[:2]
    nfreq = freq_index.shape[0]
    nband, nrow, ncol = (lax.axis_size(a) for a in ("band", "row", "col"))
    axes = ("row", "col", "band")
    line = is_line(ncol)
    place = jnp.stack([lax.axis_index(a) for a in axes]).astype(jnp.int32)

    rights, whose = gather_xor(right_pieces, "row")
    if nrow & (nrow - 1):
        table_of = lambda q, row: (q + nrow - row) % nrow
    else:
        table_of = lambda q, row: q ^ row

    def pieces(left, owner, use=None):
        slot = lambda row, col, group: table_of(owner(col), row)
        return [(left[k], (slot, use, k)) for k in range(bpiece)]

    if line:
        far = lax.ppermute(left_pieces, "col", xor_pairs(4, 2))
        near = lax.ppermute(left_pieces, "col", xor_pairs(4, 1))
        mid = lax.ppermute(left_pieces, "col", [(1, 2), (2, 1)])
        hop = lax.ppermute(far, "col", [(2, 3), (1, 0)])
        inner = lambda row, col, group: (col == 1) | (col == 2)
        outer = lambda row, col, group: (col == 0) | (col == 3)
        soon = (
            pieces(left_pieces, lambda col: col)
            + pieces(near, lambda col: col ^ 1)
            + pieces(far, lambda col: col ^ 2)
        )
        last = pieces(mid, lambda col: col ^ 3, inner) + pieces(hop, lambda col: col ^ 3, outer)
    else:
        lefts, owner_of = gather_xor(left_pieces, "col")
        last = [
            p
            for d, left in enumerate(lefts)
            for p in pieces(left, lambda col, d=d: owner_of(d, col))
        ]

    scalars = freq_index, band_energy
    ahead, amp, freq = screen(place, whose, nband, bpiece, *scalars, pole_amp, pole_freq)
    later = screen_more(place, whose, nband, nrow - 2, bpiece, *scalars, amp, freq)
    tables = []
    for d in range(nrow):
        source, first = (ahead, d) if d < 2 else (later, d - 2)
        held = [rights[d][k] for k in range(bpiece)]
        tables.append(apply_rights(source, first * bpiece, held))

    total = None
    if line:
        total = fold(place, soon, tables, None, nstate, jnp.float32)
    total = fold(place, last, tables, total, nstate, jnp.bfloat16)
    parts = lax.all_to_all(total, axes, split_axis=0, concat_axis=0, tiled=True)
    ndev = lax.axis_size(axes)
    owned = nstate // ndev
    mine = jnp.sum(parts.reshape(ndev, owned, nfreq, nstate).astype(jnp.float32), axis=0)
    return mine.transpose(1, 0, 2)


def solution(mesh):
    in_specs = (
        P(),
        P(),
        P("row", "col"),
        P("row", "col"),
        P(("col", "band"), None, "row"),
        P(("row", "band"), None, "col"),
    )
    out_specs = P(None, ("row", "col", "band"), None)

    return jax.shard_map(body, mesh=mesh, in_specs=in_specs, out_specs=out_specs, check_vma=False)
```

time: 291 us -> 70.3 us (0.24)
  waiting for transfers between devices: 215 us -> 22.6 us
  matrix products: 40.5 us -> 0 us
  Pallas kernels: 0 us -> 19.1 us
  blocking collectives: 0 us -> 16.4 us
  between operations: 13.1 us -> 0.12 us
  loops' own time: 10.7 us -> 0 us
  starting transfers between devices: 0.08 us -> 9.65 us
  local copies, waits for them, and re-layouts: 9.74 us -> 1.32 us
    psum x1 -> x0, waiting for transfers between devices: 129 us -> none  [body(): summed = lax.psum(total, ('row', 'col', 'band'))]
    all_gather x2 -> x0, waiting for transfers between devices: 84.4 us -> none  [the longest x1 48.6 us: body(): left_all = lax.all_gather(left_pieces, 'col', axis=0, tiled=True)]
    dot_general x8 -> x0, matrix products: 40.5 us -> none  [add_band(): lax.dot_general(partial_value, right_band, (((1,), (1,)), ((), ())), pref...]
    ppermute x0 -> x7, waiting for transfers between devices: none -> 22.6 us  [the longest x1 12.4 us: body(): far = lax.ppermute(left_pieces, 'col', xor_pairs(4, 2))]
    pallas_call x0 -> x8, Pallas kernels: none -> 19.1 us  [the longest x1 6.21 us: screen(): pl.pallas_call(functools.partial(screen_kernel, arrivals, nband, bpiece),...]
    all_to_all x0 -> x1, blocking collectives: none -> 16.4 us  [body(): parts = lax.all_to_all(total, axes, split_axis=0, concat_axis=0, tiled=True)]
    another operation x1 -> x0, loops' own time: 10.7 us -> none  [body(): total = lax.fori_loop(0, left_all.shape[0], step, start)]
    ppermute x0 -> x7, starting transfers between devices: none -> 9.65 us  [the longest x1 4.06 us: body(): far = lax.ppermute(left_pieces, 'col', xor_pairs(4, 2))]
  transfers between devices with their start and end apart: 3 -> 7, of which waited for: 3 -> 3; matrix products, arithmetic and copies ran while one was open for 0% -> 0% of each run, Pallas kernels for 0% -> 26%
where the time goes in v1:
time: 70.3 us; the launch traced here: 69.8 us
  waiting for transfers between devices  22.6 us (32%)
  Pallas kernels  19.1 us (27%)
  blocking collectives  16.4 us (23%)
  starting transfers between devices  9.65 us (14%)
  local copies, waits for them, and re-layouts  1.32 us (2%)
  other arithmetic  0.73 us (1%)
    all_to_all x1, blocking collectives, body(): parts = lax.all_to_all(total, axes, split_axis=0, concat_axis=0, tiled=True)  16.4 us
    ppermute x1, waiting for transfers between devices, body(): far = lax.ppermute(left_pieces, 'col', xor_pairs(4, 2))  12.4 us
    ppermute x1, waiting for transfers between devices, body(): hop = lax.ppermute(far, 'col', [(2, 3), (1, 0)])  6.73 us
    pallas_call x1, Pallas kernels, screen(): pl.pallas_call(functools.partial(screen_kernel, arrivals, nband, bpiece),...  6.21 us
    pallas_call x4, Pallas kernels, apply_rights(): pl.pallas_call(functools.partial(apply_kernel, first), in_specs=[WHOLE] *...  5.13 us
    pallas_call x1, Pallas kernels, screen_more(): pl.pallas_call(functools.partial(more_kernel, arrivals, nband, bpiece), i...  4.77 us
    ppermute x1, starting transfers between devices, body(): far = lax.ppermute(left_pieces, 'col', xor_pairs(4, 2))  4.06 us
    ppermute x3, starting transfers between devices, gather_xor(): lax.ppermute(piece, axis, xor_pairs(n, d))  3.55 us
  transfers between devices with their start and end apart: 7, of which 3 were waited for; matrix products, arithmetic and copies ran while one was open for 0% of the time, Pallas kernels for 26%

profile of v1, /device:TPU:0, one launch (start us, length us, event | category | flops | bytes accessed | tf_op | source)
XLA Modules:
  0.0 69.8 jit_solution(18096572821059794713)
XLA Ops:
  0.0 4.1 %collective-permute-start.1 = (bf16[1,256,1024]{2,1,0:T(8,128)(2,1)}, bf16[1,256,1024]{2,1,0:T(8,128)(2,1)S(1)}, u32[]{:S(2)}, u32[]{:S(2)}) collective-permute-start(bf16[1,256,1024]{2,1,0:T(8,128)(2,1)} %param.10), channel_id=1, source_target_pairs={{0,4},{2,6},{4,0},{6,2},{1,5},{3,7},{5,1},{7,3},{8,12},{10,14},{12... | collective-permute-start | bytes 1572872 | tf_op jit(solution)/shard_map/ppermute | solution.py:255
  4.1 1.5 %collective-permute-start.3 = (bf16[1,256,1024]{2,1,0:T(8,128)(2,1)}, bf16[1,256,1024]{2,1,0:T(8,128)(2,1)S(1)}, u32[]{:S(2)}, u32[]{:S(2)}) collective-permute-start(bf16[1,256,1024]{2,1,0:T(8,128)(2,1)} %param.11), channel_id=1, source_target_pairs={{0,8},{8,0},{16,24},{24,16},{1,9},{9,1},{17,25},{25,17},{2,10},{10... | collective-permute-start | bytes 1572872 | tf_op jit(solution)/shard_map/ppermute | solution.py:228
  5.6 0.7 collective-permute-start
  6.2 1.6 %collective-permute-start.4 = (bf16[1,256,1024]{2,1,0:T(8,128)(2,1)}, bf16[1,256,1024]{2,1,0:T(8,128)(2,1)S(1)}, u32[]{:S(2)}, u32[]{:S(2)}) collective-permute-start(bf16[1,256,1024]{2,1,0:T(8,128)(2,1)} %param.11), channel_id=1, source_target_pairs={{0,16},{8,24},{16,0},{24,8},{1,17},{9,25},{17,1},{25,9},{2,18},{10... | collective-permute-start | bytes 1572872 | tf_op jit(solution)/shard_map/ppermute | solution.py:228
  7.8 0.5 collective-permute-start.5
  8.3 0.1 pad_add_fusion.place_ref
  8.4 0.0 copy-start.2
  8.4 0.7 copy-done.2
  9.0 0.0 copy-start.3
  9.0 0.7 copy-done.3
  9.7 6.2 %screen.1 = (bf16[2,2,1024,1024]{3,2,1,0:T(8,128)(2,1)S(1)}, f32[1024,1024]{1,0:T(8,128)S(1)}, f32[1024,1024]{1,0:T(8,128)S(1)}) custom-call(s32[3]{0:T(128)S(1)} %pad_add_fusion.place_ref, s32[2]{0:T(128)S(1)} %copy-done.2, f32[8]{0:T(128)S(1)} %copy-done.3, f32[1024,1024]{1,0:T(8,128)} %amp_hbm.1, f32[1024,1024]{1,0:T(8,128)} %freq_hbm.1), custom_call_target="tpu_custom_call" | custom-call | flops 2147483648 | bytes 8388608 | tf_op jit(solution)/shard_map/screen/pallas_call | solution.py:92
  15.9 12.4 %collective-permute-done.1 = bf16[1,256,1024]{2,1,0:T(8,128)(2,1)S(1)} collective-permute-done((bf16[1,256,1024]{2,1,0:T(8,128)(2,1)}, bf16[1,256,1024]{2,1,0:T(8,128)(2,1)S(1)}, u32[]{:S(2)}, u32[]{:S(2)}) %collective-permute-start.1) | collective-permute-done | bytes 524320 | tf_op jit(solution)/shard_map/ppermute | solution.py:255
  28.3 0.0 copy-done.1
  28.3 0.1 collective-permute-start.6
  28.4 0.0 collective-permute-done.3
  28.4 1.3 %collective-permute-start.2 = (bf16[1,256,1024]{2,1,0:T(8,128)(2,1)S(1)}, bf16[1,256,1024]{2,1,0:T(8,128)(2,1)S(1)}, u32[]{:S(2)}, u32[]{:S(2)}) collective-permute-start(bf16[1,256,1024]{2,1,0:T(8,128)(2,1)S(1)} %collective-permute-done.1), channel_id=1, source_target_pairs={{4,6},{2,0},{5,7},{3,1},{12,14},{10,8},{13,15},{11,9},{20,22},{18,... | collective-permute-start | bytes 1572872 | tf_op jit(solution)/shard_map/ppermute | solution.py:258
  29.7 0.0 copy-start
  29.7 4.8 %more.1.ahead_ref = bf16[2,2,1024,1024]{3,2,1,0:T(8,128)(2,1)S(1)} custom-call(s32[3]{0:T(128)S(1)} %pad_add_fusion.place_ref, s32[2]{0:T(128)S(1)} %copy-done.2, f32[8]{0:T(128)S(1)} %copy-done.3, f32[1024,1024]{1,0:T(8,128)S(1)} %get-tuple-element.9.amp_ref, f32[1024,1024]{1,0:T(8,128)S(1)} %get-tuple-element.10.freq_ref), custom_call_target="tpu_custom_call" | custom-call | flops 2147483648 | bytes 8388608 | tf_op jit(solution)/shard_map/more/pallas_call | solution.py:131
  34.4 0.0 copy-done
  34.5 1.3 %apply.4.rest_3_.rest_2_ = bf16[1,1024,512]{2,1,0:T(8,128)(2,1)S(1)} custom-call(bf16[2,2,1024,1024]{3,2,1,0:T(8,128)(2,1)S(1)} %get-tuple-element.8.ahead_ref, bf16[256,1024]{1,0:T(8,128)(2,1)S(1)} %bitcast.17), custom_call_target="tpu_custom_call" | custom-call | flops 1073741824 | bytes 4194304 | tf_op jit(solution)/shard_map/apply/pallas_call | solution.py:158
  35.7 1.3 %apply.5.rest_4_.rest_3_ = bf16[1,1024,512]{2,1,0:T(8,128)(2,1)S(1)} custom-call(bf16[2,2,1024,1024]{3,2,1,0:T(8,128)(2,1)S(1)} %get-tuple-element.8.ahead_ref, bf16[256,1024]{1,0:T(8,128)(2,1)S(1)} %bitcast.21), custom_call_target="tpu_custom_call" | custom-call | flops 1073741824 | bytes 4194304 | tf_op jit(solution)/shard_map/apply/pallas_call | solution.py:158
  37.0 0.0 collective-permute-done.4
  37.0 1.3 %apply.6.rest_5_.rest_4_ = bf16[1,1024,512]{2,1,0:T(8,128)(2,1)S(1)} custom-call(bf16[2,2,1024,1024]{3,2,1,0:T(8,128)(2,1)S(1)} %more.1.ahead_ref, bf16[256,1024]{1,0:T(8,128)(2,1)S(1)} %bitcast.23), custom_call_target="tpu_custom_call" | custom-call | flops 1073741824 | bytes 4194304 | tf_op jit(solution)/shard_map/apply/pallas_call | solution.py:158
  38.3 0.0 collective-permute-done.5
  38.3 1.3 %apply.7.rest_6_.rest_5_ = bf16[1,1024,512]{2,1,0:T(8,128)(2,1)S(1)} custom-call(bf16[2,2,1024,1024]{3,2,1,0:T(8,128)(2,1)S(1)} %more.1.ahead_ref, bf16[256,1024]{1,0:T(8,128)(2,1)S(1)} %bitcast.22), custom_call_target="tpu_custom_call" | custom-call | flops 1073741824 | bytes 4194304 | tf_op jit(solution)/shard_map/apply/pallas_call | solution.py:158
  39.6 3.5 %collective-permute-done.6 = bf16[1,256,1024]{2,1,0:T(8,128)(2,1)S(1)} collective-permute-done((bf16[1,256,1024]{2,1,0:T(8,128)(2,1)S(1)}, bf16[1,256,1024]{2,1,0:T(8,128)(2,1)S(1)}, u32[]{:S(2)}, u32[]{:S(2)}) %collective-permute-start.6) | collective-permute-done | bytes 524320 | tf_op jit(solution)/shard_map/ppermute | solution.py:256
  43.1 1.9 %fold.2.rest_6_ = f32[256,512]{1,0:T(8,128)S(1)} custom-call(s32[3]{0:T(128)S(1)} %pad_add_fusion.place_ref, bf16[256,1024]{1,0:T(8,128)(2,1)S(1)} %bitcast.18, bf16[256,1024]{1,0:T(8,128)(2,1)S(1)} %bitcast.25, bf16[256,1024]{1,0:T(8,128)(2,1)S(1)} %bitcast.19, bf16[1,1024,512]{2,1,0:T(8,128)(2,1)S(1)} %apply.4.rest_3_.rest_2_, ...), custom_call_target="tpu_custom_call" | custom-call | flops 805306368 | bytes 4718592 | tf_op jit(solution)/shard_map/fold/pallas_call | solution.py:200
  45.0 0.0 collective-permute-done
  45.0 6.7 %collective-permute-done.2 = bf16[1,256,1024]{2,1,0:T(8,128)(2,1)S(1)} collective-permute-done((bf16[1,256,1024]{2,1,0:T(8,128)(2,1)S(1)}, bf16[1,256,1024]{2,1,0:T(8,128)(2,1)S(1)}, u32[]{:S(2)}, u32[]{:S(2)}) %collective-permute-start.2) | collective-permute-done | bytes 524320 | tf_op jit(solution)/shard_map/ppermute | solution.py:258
  51.8 1.1 %fold.3 = bf16[256,512]{1,0:T(8,128)(2,1)S(1)} custom-call(s32[3]{0:T(128)S(1)} %pad_add_fusion.place_ref, bf16[256,1024]{1,0:T(8,128)(2,1)S(1)} %bitcast.20, bf16[256,1024]{1,0:T(8,128)(2,1)S(1)} %bitcast.24, bf16[1,1024,512]{2,1,0:T(8,128)(2,1)S(1)} %apply.4.rest_3_.rest_2_, bf16[1,1024,512]{2,1,0:T(8,128)(2,1)S(1)} %apply.5.rest_4_.rest_3_, ...), custom_call_target="tpu_custom_call" | custom-call | flops 536870912 | bytes 3145728 | tf_op jit(solution)/shard_map/fold/pallas_call | solution.py:200
  52.8 16.4 %all_to_all.9 = bf16[32,8,512]{2,1,0:T(8,128)(2,1)S(1)} all-to-all(bf16[32,8,512]{2,1,0:T(8,128)(2,1)S(1)} %bitcast.16), channel_id=1, replica_groups=mesh['row'=4,'col'=4,'band'=2] {'row','col','band'}, dimensions={0} | all-to-all | bytes 524288 | tf_op jit(solution)/shard_map/all_to_all | solution.py:288
  69.2 0.7 convert_reduce_fusion
  (1 shorter events, 0.0 us)
Async XLA Ops:
  0.0 28.3 %collective-permute-start.1 = (bf16[1,256,1024]{2,1,0:T(8,128)(2,1)}, bf16[1,256,1024]{2,1,0:T(8,128)(2,1)S(1)}, u32[]{:S(2)}, u32[]{:S(2)}) collective-permute-start(bf16[1,256,1024]{2,1,0:T(8,128)(2,1)} %param.10), channel_id=1, source_target_pairs={{0,4},{2,6},{4,0},{6,2},{1,5},{3,7},{5,1},{7,3},{8,12},{10,14},{12... | collective-permute-start | bytes 1572872 | tf_op jit(solution)/shard_map/ppermute | solution.py:255
  4.1 24.3 %collective-permute-start.3 = (bf16[1,256,1024]{2,1,0:T(8,128)(2,1)}, bf16[1,256,1024]{2,1,0:T(8,128)(2,1)S(1)}, u32[]{:S(2)}, u32[]{:S(2)}) collective-permute-start(bf16[1,256,1024]{2,1,0:T(8,128)(2,1)} %param.11), channel_id=1, source_target_pairs={{0,8},{8,0},{16,24},{24,16},{1,9},{9,1},{17,25},{25,17},{2,10},{10... | collective-permute-start | bytes 1572872 | tf_op jit(solution)/shard_map/ppermute | solution.py:228
  5.6 39.5 %collective-permute-start = (bf16[1,256,1024]{2,1,0:T(8,128)(2,1)}, bf16[1,256,1024]{2,1,0:T(8,128)(2,1)S(1)}, u32[]{:S(2)}, u32[]{:S(2)}) collective-permute-start(bf16[1,256,1024]{2,1,0:T(8,128)(2,1)} %param.10), channel_id=1, source_target_pairs={{2,4},{4,2},{3,5},{5,3},{10,12},{12,10},{11,13},{13,11},{18,20},{2... | collective-permute-start | bytes 1572872 | tf_op jit(solution)/shard_map/ppermute | solution.py:257
  6.2 30.8 %collective-permute-start.4 = (bf16[1,256,1024]{2,1,0:T(8,128)(2,1)}, bf16[1,256,1024]{2,1,0:T(8,128)(2,1)S(1)}, u32[]{:S(2)}, u32[]{:S(2)}) collective-permute-start(bf16[1,256,1024]{2,1,0:T(8,128)(2,1)} %param.11), channel_id=1, source_target_pairs={{0,16},{8,24},{16,0},{24,8},{1,17},{9,25},{17,1},{25,9},{2,18},{10... | collective-permute-start | bytes 1572872 | tf_op jit(solution)/shard_map/ppermute | solution.py:228
  7.8 30.5 %collective-permute-start.5 = (bf16[1,256,1024]{2,1,0:T(8,128)(2,1)}, bf16[1,256,1024]{2,1,0:T(8,128)(2,1)S(1)}, u32[]{:S(2)}, u32[]{:S(2)}) collective-permute-start(bf16[1,256,1024]{2,1,0:T(8,128)(2,1)} %param.11), channel_id=1, source_target_pairs={{0,24},{8,16},{16,8},{24,0},{1,25},{9,17},{17,9},{25,1},{2,26},{10... | collective-permute-start | bytes 1572872 | tf_op jit(solution)/shard_map/ppermute | solution.py:228
  8.4 0.7 copy-start.2
  9.0 0.7 copy-start.3
  9.7 18.6 %copy-start.1 = (bf16[1,256,1024]{2,1,0:T(8,128)(2,1)S(1)}, bf16[1,256,1024]{2,1,0:T(8,128)(2,1)}, u32[]{:S(2)}) copy-start(bf16[1,256,1024]{2,1,0:T(8,128)(2,1)} %param.10) | copy-start | bytes 1572868
  28.3 14.8 %collective-permute-start.6 = (bf16[1,256,1024]{2,1,0:T(8,128)(2,1)S(1)}, bf16[1,256,1024]{2,1,0:T(8,128)(2,1)S(1)}, u32[]{:S(2)}, u32[]{:S(2)}) collective-permute-start(bf16[1,256,1024]{2,1,0:T(8,128)(2,1)S(1)} %copy-done.1), channel_id=1, source_target_pairs={{0,2},{2,0},{4,6},{6,4},{1,3},{3,1},{5,7},{7,5},{8,10},{10,8},{12,... | collective-permute-start | bytes 1572872 | tf_op jit(solution)/shard_map/ppermute | solution.py:256
  28.4 23.4 %collective-permute-start.2 = (bf16[1,256,1024]{2,1,0:T(8,128)(2,1)S(1)}, bf16[1,256,1024]{2,1,0:T(8,128)(2,1)S(1)}, u32[]{:S(2)}, u32[]{:S(2)}) collective-permute-start(bf16[1,256,1024]{2,1,0:T(8,128)(2,1)S(1)} %collective-permute-done.1), channel_id=1, source_target_pairs={{4,6},{2,0},{5,7},{3,1},{12,14},{10,8},{13,15},{11,9},{20,22},{18,... | collective-permute-start | bytes 1572872 | tf_op jit(solution)/shard_map/ppermute | solution.py:258
  29.7 4.8 %copy-start = (bf16[1,256,1024]{2,1,0:T(8,128)(2,1)S(1)}, bf16[1,256,1024]{2,1,0:T(8,128)(2,1)}, u32[]{:S(2)}) copy-start(bf16[1,256,1024]{2,1,0:T(8,128)(2,1)} %param.11) | copy-start | bytes 1572868

commit v2 on v1

--- a/solution.py
+++ b/solution.py
@@ -252,16 +252,18 @@
         return [(left[k], (slot, use, k)) for k in range(bpiece)]
 
     if line:
-        far = lax.ppermute(left_pieces, "col", xor_pairs(4, 2))
+        inward = lax.ppermute(left_pieces, "col", [(0, 2), (3, 1)])
+        outward = lax.ppermute(left_pieces, "col", [(1, 3), (2, 0)])
         near = lax.ppermute(left_pieces, "col", xor_pairs(4, 1))
         mid = lax.ppermute(left_pieces, "col", [(1, 2), (2, 1)])
-        hop = lax.ppermute(far, "col", [(2, 3), (1, 0)])
+        hop = lax.ppermute(inward, "col", [(2, 3), (1, 0)])
         inner = lambda row, col, group: (col == 1) | (col == 2)
         outer = lambda row, col, group: (col == 0) | (col == 3)
         soon = (
             pieces(left_pieces, lambda col: col)
             + pieces(near, lambda col: col ^ 1)
-            + pieces(far, lambda col: col ^ 2)
+            + pieces(inward, lambda col: col ^ 2, inner)
+            + pieces(outward, lambda col: col ^ 2, outer)
         )
         last = pieces(mid, lambda col: col ^ 3, inner) + pieces(hop, lambda col: col ^ 3, outer)
     else:

time: 70.3 us -> 70 us (level)
  starting transfers between devices: 9.65 us -> 14.7 us
  waiting for transfers between devices: 22.6 us -> 19 us
  blocking collectives: 16.4 us -> 14.5 us
    ppermute x2 -> x3, waiting for transfers between devices: 19.1 us -> 7.28 us  [the longest x1 7.27 us: body(): hop = lax.ppermute(inward, 'col', [(2, 3), (1, 0)])]
    ppermute x3, waiting for transfers between devices: 0.01 us -> 11 us  [gather_xor(): lax.ppermute(piece, axis, xor_pairs(n, d))]
    ppermute x2 -> x3, starting transfers between devices: 5.35 us -> 8.55 us  [the longest x1 5.99 us: body(): inward = lax.ppermute(left_pieces, 'col', [(0, 2), (3, 1)])]
    ppermute x1, waiting for transfers between devices: 3.45 us -> 0.66 us  [body(): near = lax.ppermute(left_pieces, 'col', xor_pairs(4, 1))]
    all_to_all x1, blocking collectives: 16.4 us -> 14.5 us  [body(): parts = lax.all_to_all(total, axes, split_axis=0, concat_axis=0, tiled=True)]
    ppermute x1, starting transfers between devices: 0.07 us -> 1.87 us  [body(): near = lax.ppermute(left_pieces, 'col', xor_pairs(4, 1))]
  transfers between devices with their start and end apart: 7 -> 8, of which waited for: 3 -> 4; matrix products, arithmetic and copies ran while one was open for 0% -> 0% of each run, Pallas kernels for 26% -> 26%
where the time goes in v2:
time: 70 us; the launch traced here: 69.6 us
  Pallas kernels  19.2 us (27%)
  waiting for transfers between devices  19 us (27%)
  starting transfers between devices  14.7 us (21%)
  blocking collectives  14.5 us (21%)
  local copies, waits for them, and re-layouts  1.32 us (2%)
  other arithmetic  0.73 us (1%)
    all_to_all x1, blocking collectives, body(): parts = lax.all_to_all(total, axes, split_axis=0, concat_axis=0, tiled=True)  14.5 us
    ppermute x3, waiting for transfers between devices, gather_xor(): lax.ppermute(piece, axis, xor_pairs(n, d))  11 us
    ppermute x1, waiting for transfers between devices, body(): hop = lax.ppermute(inward, 'col', [(2, 3), (1, 0)])  7.27 us
    pallas_call x1, Pallas kernels, screen(): pl.pallas_call(functools.partial(screen_kernel, arrivals, nband, bpiece),...  6.21 us
    ppermute x1, starting transfers between devices, body(): inward = lax.ppermute(left_pieces, 'col', [(0, 2), (3, 1)])  5.99 us
    pallas_call x4, Pallas kernels, apply_rights(): pl.pallas_call(functools.partial(apply_kernel, first), in_specs=[WHOLE] *...  5.14 us
    pallas_call x1, Pallas kernels, screen_more(): pl.pallas_call(functools.partial(more_kernel, arrivals, nband, bpiece), i...  4.77 us
    ppermute x3, starting transfers between devices, gather_xor(): lax.ppermute(piece, axis, xor_pairs(n, d))  3.62 us
  transfers between devices with their start and end apart: 8, of which 4 were waited for; matrix products, arithmetic and copies ran while one was open for 0% of the time, Pallas kernels for 26%

profile of v2, /device:TPU:0, one launch (start us, length us, event | category | flops | bytes accessed | tf_op | source)
XLA Modules:
  0.0 69.6 jit_solution(2773171214572370232)
XLA Ops:
  0.0 6.0 %collective-permute-start.1 = (bf16[1,256,1024]{2,1,0:T(8,128)(2,1)}, bf16[1,256,1024]{2,1,0:T(8,128)(2,1)S(1)}, u32[]{:S(2)}, u32[]{:S(2)}) collective-permute-start(bf16[1,256,1024]{2,1,0:T(8,128)(2,1)} %param.10), channel_id=1, source_target_pairs={{0,4},{6,2},{1,5},{7,3},{8,12},{14,10},{9,13},{15,11},{16,20},{22,... | collective-permute-start | bytes 1572872 | tf_op jit(solution)/shard_map/ppermute | solution.py:255
  6.0 1.6 %collective-permute-start.3 = (bf16[1,256,1024]{2,1,0:T(8,128)(2,1)}, bf16[1,256,1024]{2,1,0:T(8,128)(2,1)S(1)}, u32[]{:S(2)}, u32[]{:S(2)}) collective-permute-start(bf16[1,256,1024]{2,1,0:T(8,128)(2,1)} %param.11), channel_id=1, source_target_pairs={{0,8},{8,0},{16,24},{24,16},{1,9},{9,1},{17,25},{25,17},{2,10},{10... | collective-permute-start | bytes 1572872 | tf_op jit(solution)/shard_map/ppermute | solution.py:228
  7.6 1.5 %collective-permute-start.4 = (bf16[1,256,1024]{2,1,0:T(8,128)(2,1)}, bf16[1,256,1024]{2,1,0:T(8,128)(2,1)S(1)}, u32[]{:S(2)}, u32[]{:S(2)}) collective-permute-start(bf16[1,256,1024]{2,1,0:T(8,128)(2,1)} %param.11), channel_id=1, source_target_pairs={{0,16},{8,24},{16,0},{24,8},{1,17},{9,25},{17,1},{25,9},{2,18},{10... | collective-permute-start | bytes 1572872 | tf_op jit(solution)/shard_map/ppermute | solution.py:228
  9.1 0.7 collective-permute-start
  9.8 0.5 collective-permute-start.5
  10.3 0.1 pad_add_fusion.place_ref
  10.4 0.7 copy-done.2
  11.0 0.7 copy-done.3
  11.7 6.2 %screen.1 = (bf16[2,2,1024,1024]{3,2,1,0:T(8,128)(2,1)S(1)}, f32[1024,1024]{1,0:T(8,128)S(1)}, f32[1024,1024]{1,0:T(8,128)S(1)}) custom-call(s32[3]{0:T(128)S(1)} %pad_add_fusion.place_ref, s32[2]{0:T(128)S(1)} %copy-done.2, f32[8]{0:T(128)S(1)} %copy-done.3, f32[1024,1024]{1,0:T(8,128)} %amp_hbm.1, f32[1024,1024]{1,0:T(8,128)} %freq_hbm.1), custom_call_target="tpu_custom_call" | custom-call | flops 2147483648 | bytes 8388608 | tf_op jit(solution)/shard_map/screen/pallas_call | solution.py:92
  17.9 0.0 collective-permute-done.1
  17.9 0.0 copy-done.1
  17.9 1.9 %collective-permute-start.6 = (bf16[1,256,1024]{2,1,0:T(8,128)(2,1)S(1)}, bf16[1,256,1024]{2,1,0:T(8,128)(2,1)S(1)}, u32[]{:S(2)}, u32[]{:S(2)}) collective-permute-start(bf16[1,256,1024]{2,1,0:T(8,128)(2,1)S(1)} %copy-done.1), channel_id=1, source_target_pairs={{0,2},{2,0},{4,6},{6,4},{1,3},{3,1},{5,7},{7,5},{8,10},{10,8},{12,... | collective-permute-start | bytes 1572872 | tf_op jit(solution)/shard_map/ppermute | solution.py:257
  19.8 1.3 %collective-permute-done.3 = bf16[1,256,1024]{2,1,0:T(8,128)(2,1)S(1)} collective-permute-done((bf16[1,256,1024]{2,1,0:T(8,128)(2,1)}, bf16[1,256,1024]{2,1,0:T(8,128)(2,1)S(1)}, u32[]{:S(2)}, u32[]{:S(2)}) %collective-permute-start.3) | collective-permute-done | bytes 524320 | tf_op jit(solution)/shard_map/ppermute | solution.py:228
  21.1 1.3 %collective-permute-start.7 = (bf16[1,256,1024]{2,1,0:T(8,128)(2,1)S(1)}, bf16[1,256,1024]{2,1,0:T(8,128)(2,1)S(1)}, u32[]{:S(2)}, u32[]{:S(2)}) collective-permute-start(bf16[1,256,1024]{2,1,0:T(8,128)(2,1)S(1)} %copy-done.1), channel_id=1, source_target_pairs={{2,6},{4,0},{3,7},{5,1},{10,14},{12,8},{11,15},{13,9},{18,22},{20,... | collective-permute-start | bytes 1572872 | tf_op jit(solution)/shard_map/ppermute | solution.py:256
  22.4 9.7 %collective-permute-done.4 = bf16[1,256,1024]{2,1,0:T(8,128)(2,1)S(1)} collective-permute-done((bf16[1,256,1024]{2,1,0:T(8,128)(2,1)}, bf16[1,256,1024]{2,1,0:T(8,128)(2,1)S(1)}, u32[]{:S(2)}, u32[]{:S(2)}) %collective-permute-start.4) | collective-permute-done | bytes 524320 | tf_op jit(solution)/shard_map/ppermute | solution.py:228
  32.1 1.3 %collective-permute-start.2 = (bf16[1,256,1024]{2,1,0:T(8,128)(2,1)S(1)}, bf16[1,256,1024]{2,1,0:T(8,128)(2,1)S(1)}, u32[]{:S(2)}, u32[]{:S(2)}) collective-permute-start(bf16[1,256,1024]{2,1,0:T(8,128)(2,1)S(1)} %collective-permute-done.1), channel_id=1, source_target_pairs={{4,6},{2,0},{5,7},{3,1},{12,14},{10,8},{13,15},{11,9},{20,22},{18,... | collective-permute-start | bytes 1572872 | tf_op jit(solution)/shard_map/ppermute | solution.py:259
  33.4 0.0 copy-start
  33.4 4.8 %more.1.ahead_ref = bf16[2,2,1024,1024]{3,2,1,0:T(8,128)(2,1)S(1)} custom-call(s32[3]{0:T(128)S(1)} %pad_add_fusion.place_ref, s32[2]{0:T(128)S(1)} %copy-done.2, f32[8]{0:T(128)S(1)} %copy-done.3, f32[1024,1024]{1,0:T(8,128)S(1)} %get-tuple-element.9.amp_ref, f32[1024,1024]{1,0:T(8,128)S(1)} %get-tuple-element.10.freq_ref), custom_call_target="tpu_custom_call" | custom-call | flops 2147483648 | bytes 8388608 | tf_op jit(solution)/shard_map/more/pallas_call | solution.py:131
  38.2 0.0 copy-done
  38.2 1.3 %apply.4.rest_4_.rest_2_ = bf16[1,1024,512]{2,1,0:T(8,128)(2,1)S(1)} custom-call(bf16[2,2,1024,1024]{3,2,1,0:T(8,128)(2,1)S(1)} %get-tuple-element.8.ahead_ref, bf16[256,1024]{1,0:T(8,128)(2,1)S(1)} %bitcast.18), custom_call_target="tpu_custom_call" | custom-call | flops 1073741824 | bytes 4194304 | tf_op jit(solution)/shard_map/apply/pallas_call | solution.py:158
  39.5 1.3 %apply.5.rest_5_.rest_3_ = bf16[1,1024,512]{2,1,0:T(8,128)(2,1)S(1)} custom-call(bf16[2,2,1024,1024]{3,2,1,0:T(8,128)(2,1)S(1)} %get-tuple-element.8.ahead_ref, bf16[256,1024]{1,0:T(8,128)(2,1)S(1)} %bitcast.20), custom_call_target="tpu_custom_call" | custom-call | flops 1073741824 | bytes 4194304 | tf_op jit(solution)/shard_map/apply/pallas_call | solution.py:158
  40.8 1.3 %apply.6.rest_6_.rest_4_ = bf16[1,1024,512]{2,1,0:T(8,128)(2,1)S(1)} custom-call(bf16[2,2,1024,1024]{3,2,1,0:T(8,128)(2,1)S(1)} %more.1.ahead_ref, bf16[256,1024]{1,0:T(8,128)(2,1)S(1)} %bitcast.21), custom_call_target="tpu_custom_call" | custom-call | flops 1073741824 | bytes 4194304 | tf_op jit(solution)/shard_map/apply/pallas_call | solution.py:158
  42.1 0.0 collective-permute-done.5
  42.1 1.3 %apply.7.rest_7_.rest_5_ = bf16[1,1024,512]{2,1,0:T(8,128)(2,1)S(1)} custom-call(bf16[2,2,1024,1024]{3,2,1,0:T(8,128)(2,1)S(1)} %more.1.ahead_ref, bf16[256,1024]{1,0:T(8,128)(2,1)S(1)} %bitcast.22), custom_call_target="tpu_custom_call" | custom-call | flops 1073741824 | bytes 4194304 | tf_op jit(solution)/shard_map/apply/pallas_call | solution.py:158
  43.4 0.7 collective-permute-done.6
  44.0 0.0 collective-permute-done.7
  44.0 2.0 %fold.2.rest_6_ = f32[256,512]{1,0:T(8,128)S(1)} custom-call(s32[3]{0:T(128)S(1)} %pad_add_fusion.place_ref, bf16[256,1024]{1,0:T(8,128)(2,1)S(1)} %bitcast.24, bf16[256,1024]{1,0:T(8,128)(2,1)S(1)} %bitcast.26, bf16[256,1024]{1,0:T(8,128)(2,1)S(1)} %bitcast.25, bf16[256,1024]{1,0:T(8,128)(2,1)S(1)} %bitcast.27, ...), custom_call_target="tpu_custom_call" | custom-call | flops 1073741824 | bytes 6291456 | tf_op jit(solution)/shard_map/fold/pallas_call | solution.py:200
  46.0 0.0 collective-permute-done
  46.0 7.3 %collective-permute-done.2 = bf16[1,256,1024]{2,1,0:T(8,128)(2,1)S(1)} collective-permute-done((bf16[1,256,1024]{2,1,0:T(8,128)(2,1)S(1)}, bf16[1,256,1024]{2,1,0:T(8,128)(2,1)S(1)}, u32[]{:S(2)}, u32[]{:S(2)}) %collective-permute-start.2) | collective-permute-done | bytes 524320 | tf_op jit(solution)/shard_map/ppermute | solution.py:259
  53.3 1.1 %fold.3 = bf16[256,512]{1,0:T(8,128)(2,1)S(1)} custom-call(s32[3]{0:T(128)S(1)} %pad_add_fusion.place_ref, bf16[256,1024]{1,0:T(8,128)(2,1)S(1)} %bitcast.19, bf16[256,1024]{1,0:T(8,128)(2,1)S(1)} %bitcast.23, bf16[1,1024,512]{2,1,0:T(8,128)(2,1)S(1)} %apply.4.rest_4_.rest_2_, bf16[1,1024,512]{2,1,0:T(8,128)(2,1)S(1)} %apply.5.rest_5_.rest_3_, ...), custom_call_target="tpu_custom_call" | custom-call | flops 536870912 | bytes 3145728 | tf_op jit(solution)/shard_map/fold/pallas_call | solution.py:200
  54.4 14.5 %all_to_all.9 = bf16[32,8,512]{2,1,0:T(8,128)(2,1)S(1)} all-to-all(bf16[32,8,512]{2,1,0:T(8,128)(2,1)S(1)} %bitcast.17), channel_id=1, replica_groups=mesh['row'=4,'col'=4,'band'=2] {'row','col','band'}, dimensions={0} | all-to-all | bytes 524288 | tf_op jit(solution)/shard_map/all_to_all | solution.py:290
  68.9 0.7 convert_reduce_fusion
  (3 shorter events, 0.0 us)
Async XLA Ops:
  0.0 17.9 %collective-permute-start.1 = (bf16[1,256,1024]{2,1,0:T(8,128)(2,1)}, bf16[1,256,1024]{2,1,0:T(8,128)(2,1)S(1)}, u32[]{:S(2)}, u32[]{:S(2)}) collective-permute-start(bf16[1,256,1024]{2,1,0:T(8,128)(2,1)} %param.10), channel_id=1, source_target_pairs={{0,4},{6,2},{1,5},{7,3},{8,12},{14,10},{9,13},{15,11},{16,20},{22,... | collective-permute-start | bytes 1572872 | tf_op jit(solution)/shard_map/ppermute | solution.py:255
  6.0 15.1 %collective-permute-start.3 = (bf16[1,256,1024]{2,1,0:T(8,128)(2,1)}, bf16[1,256,1024]{2,1,0:T(8,128)(2,1)S(1)}, u32[]{:S(2)}, u32[]{:S(2)}) collective-permute-start(bf16[1,256,1024]{2,1,0:T(8,128)(2,1)} %param.11), channel_id=1, source_target_pairs={{0,8},{8,0},{16,24},{24,16},{1,9},{9,1},{17,25},{25,17},{2,10},{10... | collective-permute-start | bytes 1572872 | tf_op jit(solution)/shard_map/ppermute | solution.py:228
  7.6 24.5 %collective-permute-start.4 = (bf16[1,256,1024]{2,1,0:T(8,128)(2,1)}, bf16[1,256,1024]{2,1,0:T(8,128)(2,1)S(1)}, u32[]{:S(2)}, u32[]{:S(2)}) collective-permute-start(bf16[1,256,1024]{2,1,0:T(8,128)(2,1)} %param.11), channel_id=1, source_target_pairs={{0,16},{8,24},{16,0},{24,8},{1,17},{9,25},{17,1},{25,9},{2,18},{10... | collective-permute-start | bytes 1572872 | tf_op jit(solution)/shard_map/ppermute | solution.py:228
  9.1 36.9 %collective-permute-start = (bf16[1,256,1024]{2,1,0:T(8,128)(2,1)}, bf16[1,256,1024]{2,1,0:T(8,128)(2,1)S(1)}, u32[]{:S(2)}, u32[]{:S(2)}) collective-permute-start(bf16[1,256,1024]{2,1,0:T(8,128)(2,1)} %param.10), channel_id=1, source_target_pairs={{2,4},{4,2},{3,5},{5,3},{10,12},{12,10},{11,13},{13,11},{18,20},{2... | collective-permute-start | bytes 1572872 | tf_op jit(solution)/shard_map/ppermute | solution.py:258
  9.8 32.3 %collective-permute-start.5 = (bf16[1,256,1024]{2,1,0:T(8,128)(2,1)}, bf16[1,256,1024]{2,1,0:T(8,128)(2,1)S(1)}, u32[]{:S(2)}, u32[]{:S(2)}) collective-permute-start(bf16[1,256,1024]{2,1,0:T(8,128)(2,1)} %param.11), channel_id=1, source_target_pairs={{0,24},{8,16},{16,8},{24,0},{1,25},{9,17},{17,9},{25,1},{2,26},{10... | collective-permute-start | bytes 1572872 | tf_op jit(solution)/shard_map/ppermute | solution.py:228
  10.4 0.7 copy-start.2
  11.0 0.7 copy-start.3
  11.7 6.2 %copy-start.1 = (bf16[1,256,1024]{2,1,0:T(8,128)(2,1)S(1)}, bf16[1,256,1024]{2,1,0:T(8,128)(2,1)}, u32[]{:S(2)}) copy-start(bf16[1,256,1024]{2,1,0:T(8,128)(2,1)} %param.10) | copy-start | bytes 1572868
  17.9 26.1 %collective-permute-start.6 = (bf16[1,256,1024]{2,1,0:T(8,128)(2,1)S(1)}, bf16[1,256,1024]{2,1,0:T(8,128)(2,1)S(1)}, u32[]{:S(2)}, u32[]{:S(2)}) collective-permute-start(bf16[1,256,1024]{2,1,0:T(8,128)(2,1)S(1)} %copy-done.1), channel_id=1, source_target_pairs={{0,2},{2,0},{4,6},{6,4},{1,3},{3,1},{5,7},{7,5},{8,10},{10,8},{12,... | collective-permute-start | bytes 1572872 | tf_op jit(solution)/shard_map/ppermute | solution.py:257
  21.1 23.0 %collective-permute-start.7 = (bf16[1,256,1024]{2,1,0:T(8,128)(2,1)S(1)}, bf16[1,256,1024]{2,1,0:T(8,128)(2,1)S(1)}, u32[]{:S(2)}, u32[]{:S(2)}) collective-permute-start(bf16[1,256,1024]{2,1,0:T(8,128)(2,1)S(1)} %copy-done.1), channel_id=1, source_target_pairs={{2,6},{4,0},{3,7},{5,1},{10,14},{12,8},{11,15},{13,9},{18,22},{20,... | collective-permute-start | bytes 1572872 | tf_op jit(solution)/shard_map/ppermute | solution.py:256
  32.1 21.2 %collective-permute-start.2 = (bf16[1,256,1024]{2,1,0:T(8,128)(2,1)S(1)}, bf16[1,256,1024]{2,1,0:T(8,128)(2,1)S(1)}, u32[]{:S(2)}, u32[]{:S(2)}) collective-permute-start(bf16[1,256,1024]{2,1,0:T(8,128)(2,1)S(1)} %collective-permute-done.1), channel_id=1, source_target_pairs={{4,6},{2,0},{5,7},{3,1},{12,14},{10,8},{13,15},{11,9},{20,22},{18,... | collective-permute-start | bytes 1572872 | tf_op jit(solution)/shard_map/ppermute | solution.py:259
  33.4 4.8 %copy-start = (bf16[1,256,1024]{2,1,0:T(8,128)(2,1)S(1)}, bf16[1,256,1024]{2,1,0:T(8,128)(2,1)}, u32[]{:S(2)}) copy-start(bf16[1,256,1024]{2,1,0:T(8,128)(2,1)} %param.11) | copy-start | bytes 1572868

commit v3 on v2

--- a/solution.py
+++ b/solution.py
@@ -170,13 +170,13 @@
     )(ahead, *rights)
 
 
-def fold_kernel(slots, ntables, has_init, place_ref, *rest):
+def fold_kernel(slots, ntables, has_init, *rest):
     count = len(slots)
     lefts = rest[:count]
     tables = rest[count : count + ntables]
     out_ref, acc = rest[-2], rest[-1]
     acc[...] = rest[-3][...] if has_init else jnp.zeros_like(acc)
-    here = [place_ref[i] for i in range(3)]
+    here = [lax.axis_index(a) for a in ("row", "col", "band")]
     for left_ref, (slot_of, use_of, k) in zip(lefts, slots):
         slot = slot_of(*here)
         for at, table_ref in enumerate(tables):
@@ -191,15 +191,15 @@
     out_ref[...] = acc[...].astype(out_ref.dtype)
 
 
-def fold(place, pieces, tables, init, nstate, dtype):
+def fold(pieces, tables, init, nstate, dtype):
     lefts, slots = zip(*pieces)
     g, width = tables[0].shape[1:]
-    args = [place, *lefts, *tables]
+    args = [*lefts, *tables]
     if init is not None:
         args.append(init)
     return pl.pallas_call(
         functools.partial(fold_kernel, slots, len(tables), init is not None),
-        in_specs=[SCALARS] + [WHOLE] * (len(args) - 1),
+        in_specs=[WHOLE] * len(args),
         out_specs=WHOLE,
         scratch_shapes=[pltpu.VMEM((nstate, width), jnp.float32)],
         out_shape=jax.ShapeDtypeStruct((nstate, width), dtype),
@@ -285,8 +285,8 @@
 
     total = None
     if line:
-        total = fold(place, soon, tables, None, nstate, jnp.float32)
-    total = fold(place, last, tables, total, nstate, jnp.bfloat16)
+        total = fold(soon, tables, None, nstate, jnp.float32)
+    total = fold(last, tables, total, nstate, jnp.bfloat16)
     parts = lax.all_to_all(total, axes, split_axis=0, concat_axis=0, tiled=True)
     ndev = lax.axis_size(axes)
     owned = nstate // ndev

time: 70 us -> 69.5 us (level)
  Pallas kernels: 19.2 us -> 18.1 us
    pallas_call x2, Pallas kernels: 3.03 us -> 1.95 us  [fold(): pl.pallas_call(functools.partial(fold_kernel, slots, len(tables), init is...]
  transfers between devices with their start and end apart: 8 -> 8, of which waited for: 4 -> 4; matrix products, arithmetic and copies ran while one was open for 0% -> 0% of each run, Pallas kernels for 26% -> 25%
where the time goes in v3:
time: 69.5 us; the launch traced here: 69 us
  waiting for transfers between devices  19.5 us (28%)
  Pallas kernels  18.1 us (26%)
  starting transfers between devices  14.7 us (21%)
  blocking collectives  14.5 us (21%)
  local copies, waits for them, and re-layouts  1.32 us (2%)
  other arithmetic  0.73 us (1%)
    all_to_all x1, blocking collectives, body(): parts = lax.all_to_all(total, axes, split_axis=0, concat_axis=0, tiled=True)  14.5 us
    ppermute x3, waiting for transfers between devices, gather_xor(): lax.ppermute(piece, axis, xor_pairs(n, d))  11 us
    ppermute x1, waiting for transfers between devices, body(): hop = lax.ppermute(inward, 'col', [(2, 3), (1, 0)])  7.81 us
    pallas_call x1, Pallas kernels, screen(): pl.pallas_call(functools.partial(screen_kernel, arrivals, nband, bpiece),...  6.21 us
    ppermute x1, starting transfers between devices, body(): inward = lax.ppermute(left_pieces, 'col', [(0, 2), (3, 1)])  5.99 us
    pallas_call x4, Pallas kernels, apply_rights(): pl.pallas_call(functools.partial(apply_kernel, first), in_specs=[WHOLE] *...  5.14 us
    pallas_call x1, Pallas kernels, screen_more(): pl.pallas_call(functools.partial(more_kernel, arrivals, nband, bpiece), i...  4.77 us
    ppermute x3, starting transfers between devices, gather_xor(): lax.ppermute(piece, axis, xor_pairs(n, d))  3.62 us
  transfers between devices with their start and end apart: 8, of which 4 were waited for; matrix products, arithmetic and copies ran while one was open for 0% of the time, Pallas kernels for 25%

profile of v3, /device:TPU:0, one launch (start us, length us, event | category | flops | bytes accessed | tf_op | source)
XLA Modules:
  0.0 69.0 jit_solution(12058547074598590951)
XLA Ops:
  0.0 6.0 %collective-permute-start.1 = (bf16[1,256,1024]{2,1,0:T(8,128)(2,1)}, bf16[1,256,1024]{2,1,0:T(8,128)(2,1)S(1)}, u32[]{:S(2)}, u32[]{:S(2)}) collective-permute-start(bf16[1,256,1024]{2,1,0:T(8,128)(2,1)} %param.10), channel_id=1, source_target_pairs={{0,4},{6,2},{1,5},{7,3},{8,12},{14,10},{9,13},{15,11},{16,20},{22,... | collective-permute-start | bytes 1572872 | tf_op jit(solution)/shard_map/ppermute | solution.py:255
  6.0 1.6 %collective-permute-start.3 = (bf16[1,256,1024]{2,1,0:T(8,128)(2,1)}, bf16[1,256,1024]{2,1,0:T(8,128)(2,1)S(1)}, u32[]{:S(2)}, u32[]{:S(2)}) collective-permute-start(bf16[1,256,1024]{2,1,0:T(8,128)(2,1)} %param.11), channel_id=1, source_target_pairs={{0,8},{8,0},{16,24},{24,16},{1,9},{9,1},{17,25},{25,17},{2,10},{10... | collective-permute-start | bytes 1572872 | tf_op jit(solution)/shard_map/ppermute | solution.py:228
  7.6 1.5 %collective-permute-start.4 = (bf16[1,256,1024]{2,1,0:T(8,128)(2,1)}, bf16[1,256,1024]{2,1,0:T(8,128)(2,1)S(1)}, u32[]{:S(2)}, u32[]{:S(2)}) collective-permute-start(bf16[1,256,1024]{2,1,0:T(8,128)(2,1)} %param.11), channel_id=1, source_target_pairs={{0,16},{8,24},{16,0},{24,8},{1,17},{9,25},{17,1},{25,9},{2,18},{10... | collective-permute-start | bytes 1572872 | tf_op jit(solution)/shard_map/ppermute | solution.py:228
  9.1 0.7 collective-permute-start
  9.8 0.5 collective-permute-start.5
  10.3 0.1 pad_add_fusion.place_ref
  10.4 0.7 copy-done.2
  11.0 0.7 copy-done.3
  11.7 6.2 %screen.1 = (bf16[2,2,1024,1024]{3,2,1,0:T(8,128)(2,1)S(1)}, f32[1024,1024]{1,0:T(8,128)S(1)}, f32[1024,1024]{1,0:T(8,128)S(1)}) custom-call(s32[3]{0:T(128)S(1)} %pad_add_fusion.place_ref, s32[2]{0:T(128)S(1)} %copy-done.2, f32[8]{0:T(128)S(1)} %copy-done.3, f32[1024,1024]{1,0:T(8,128)} %amp_hbm.1, f32[1024,1024]{1,0:T(8,128)} %freq_hbm.1), custom_call_target="tpu_custom_call" | custom-call | flops 2147483648 | bytes 8388608 | tf_op jit(solution)/shard_map/screen/pallas_call | solution.py:92
  17.9 0.0 collective-permute-done.1
  17.9 0.0 copy-done.1
  17.9 1.9 %collective-permute-start.6 = (bf16[1,256,1024]{2,1,0:T(8,128)(2,1)S(1)}, bf16[1,256,1024]{2,1,0:T(8,128)(2,1)S(1)}, u32[]{:S(2)}, u32[]{:S(2)}) collective-permute-start(bf16[1,256,1024]{2,1,0:T(8,128)(2,1)S(1)} %copy-done.1), channel_id=1, source_target_pairs={{0,2},{2,0},{4,6},{6,4},{1,3},{3,1},{5,7},{7,5},{8,10},{10,8},{12,... | collective-permute-start | bytes 1572872 | tf_op jit(solution)/shard_map/ppermute | solution.py:257
  19.8 1.3 %collective-permute-done.3 = bf16[1,256,1024]{2,1,0:T(8,128)(2,1)S(1)} collective-permute-done((bf16[1,256,1024]{2,1,0:T(8,128)(2,1)}, bf16[1,256,1024]{2,1,0:T(8,128)(2,1)S(1)}, u32[]{:S(2)}, u32[]{:S(2)}) %collective-permute-start.3) | collective-permute-done | bytes 524320 | tf_op jit(solution)/shard_map/ppermute | solution.py:228
  21.1 1.3 %collective-permute-start.7 = (bf16[1,256,1024]{2,1,0:T(8,128)(2,1)S(1)}, bf16[1,256,1024]{2,1,0:T(8,128)(2,1)S(1)}, u32[]{:S(2)}, u32[]{:S(2)}) collective-permute-start(bf16[1,256,1024]{2,1,0:T(8,128)(2,1)S(1)} %copy-done.1), channel_id=1, source_target_pairs={{2,6},{4,0},{3,7},{5,1},{10,14},{12,8},{11,15},{13,9},{18,22},{20,... | collective-permute-start | bytes 1572872 | tf_op jit(solution)/shard_map/ppermute | solution.py:256
  22.4 9.7 %collective-permute-done.4 = bf16[1,256,1024]{2,1,0:T(8,128)(2,1)S(1)} collective-permute-done((bf16[1,256,1024]{2,1,0:T(8,128)(2,1)}, bf16[1,256,1024]{2,1,0:T(8,128)(2,1)S(1)}, u32[]{:S(2)}, u32[]{:S(2)}) %collective-permute-start.4) | collective-permute-done | bytes 524320 | tf_op jit(solution)/shard_map/ppermute | solution.py:228
  32.1 1.3 %collective-permute-start.2 = (bf16[1,256,1024]{2,1,0:T(8,128)(2,1)S(1)}, bf16[1,256,1024]{2,1,0:T(8,128)(2,1)S(1)}, u32[]{:S(2)}, u32[]{:S(2)}) collective-permute-start(bf16[1,256,1024]{2,1,0:T(8,128)(2,1)S(1)} %collective-permute-done.1), channel_id=1, source_target_pairs={{4,6},{2,0},{5,7},{3,1},{12,14},{10,8},{13,15},{11,9},{20,22},{18,... | collective-permute-start | bytes 1572872 | tf_op jit(solution)/shard_map/ppermute | solution.py:259
  33.4 0.0 copy-start
  33.4 4.8 %more.1.ahead_ref = bf16[2,2,1024,1024]{3,2,1,0:T(8,128)(2,1)S(1)} custom-call(s32[3]{0:T(128)S(1)} %pad_add_fusion.place_ref, s32[2]{0:T(128)S(1)} %copy-done.2, f32[8]{0:T(128)S(1)} %copy-done.3, f32[1024,1024]{1,0:T(8,128)S(1)} %get-tuple-element.9.amp_ref, f32[1024,1024]{1,0:T(8,128)S(1)} %get-tuple-element.10.freq_ref), custom_call_target="tpu_custom_call" | custom-call | flops 2147483648 | bytes 8388608 | tf_op jit(solution)/shard_map/more/pallas_call | solution.py:131
  38.2 0.0 copy-done
  38.2 1.3 %apply.4.rest_4_.rest_2_ = bf16[1,1024,512]{2,1,0:T(8,128)(2,1)S(1)} custom-call(bf16[2,2,1024,1024]{3,2,1,0:T(8,128)(2,1)S(1)} %get-tuple-element.8.ahead_ref, bf16[256,1024]{1,0:T(8,128)(2,1)S(1)} %bitcast.18), custom_call_target="tpu_custom_call" | custom-call | flops 1073741824 | bytes 4194304 | tf_op jit(solution)/shard_map/apply/pallas_call | solution.py:158
  39.5 1.3 %apply.5.rest_5_.rest_3_ = bf16[1,1024,512]{2,1,0:T(8,128)(2,1)S(1)} custom-call(bf16[2,2,1024,1024]{3,2,1,0:T(8,128)(2,1)S(1)} %get-tuple-element.8.ahead_ref, bf16[256,1024]{1,0:T(8,128)(2,1)S(1)} %bitcast.20), custom_call_target="tpu_custom_call" | custom-call | flops 1073741824 | bytes 4194304 | tf_op jit(solution)/shard_map/apply/pallas_call | solution.py:158
  40.8 1.3 %apply.6.rest_6_.rest_4_ = bf16[1,1024,512]{2,1,0:T(8,128)(2,1)S(1)} custom-call(bf16[2,2,1024,1024]{3,2,1,0:T(8,128)(2,1)S(1)} %more.1.ahead_ref, bf16[256,1024]{1,0:T(8,128)(2,1)S(1)} %bitcast.21), custom_call_target="tpu_custom_call" | custom-call | flops 1073741824 | bytes 4194304 | tf_op jit(solution)/shard_map/apply/pallas_call | solution.py:158
  42.1 0.0 collective-permute-done.5
  42.1 1.3 %apply.7.rest_7_.rest_5_ = bf16[1,1024,512]{2,1,0:T(8,128)(2,1)S(1)} custom-call(bf16[2,2,1024,1024]{3,2,1,0:T(8,128)(2,1)S(1)} %more.1.ahead_ref, bf16[256,1024]{1,0:T(8,128)(2,1)S(1)} %bitcast.22), custom_call_target="tpu_custom_call" | custom-call | flops 1073741824 | bytes 4194304 | tf_op jit(solution)/shard_map/apply/pallas_call | solution.py:158
  43.4 0.7 collective-permute-done.6
  44.0 0.0 collective-permute-done.7
  44.0 1.4 %fold.2.rest_6_ = f32[256,512]{1,0:T(8,128)S(1)} custom-call(bf16[256,1024]{1,0:T(8,128)(2,1)S(1)} %bitcast.24, bf16[256,1024]{1,0:T(8,128)(2,1)S(1)} %bitcast.26, bf16[256,1024]{1,0:T(8,128)(2,1)S(1)} %bitcast.25, bf16[256,1024]{1,0:T(8,128)(2,1)S(1)} %bitcast.27, bf16[1,1024,512]{2,1,0:T(8,128)(2,1)S(1)} %apply.4.rest_4_.rest_2_, ...), custom_call_target="tpu_custom_call" | custom-call | flops 1073741824 | bytes 6291456 | tf_op jit(solution)/shard_map/fold/pallas_call | solution.py:200
  45.5 0.0 collective-permute-done
  45.5 7.8 %collective-permute-done.2 = bf16[1,256,1024]{2,1,0:T(8,128)(2,1)S(1)} collective-permute-done((bf16[1,256,1024]{2,1,0:T(8,128)(2,1)S(1)}, bf16[1,256,1024]{2,1,0:T(8,128)(2,1)S(1)}, u32[]{:S(2)}, u32[]{:S(2)}) %collective-permute-start.2) | collective-permute-done | bytes 524320 | tf_op jit(solution)/shard_map/ppermute | solution.py:259
  53.3 0.5 fold.3
  53.8 14.5 %all_to_all.9 = bf16[32,8,512]{2,1,0:T(8,128)(2,1)S(1)} all-to-all(bf16[32,8,512]{2,1,0:T(8,128)(2,1)S(1)} %bitcast.17), channel_id=1, replica_groups=mesh['row'=4,'col'=4,'band'=2] {'row','col','band'}, dimensions={0} | all-to-all | bytes 524288 | tf_op jit(solution)/shard_map/all_to_all | solution.py:290
  68.4 0.7 convert_reduce_fusion
  (3 shorter events, 0.0 us)
Async XLA Ops:
  0.0 17.9 %collective-permute-start.1 = (bf16[1,256,1024]{2,1,0:T(8,128)(2,1)}, bf16[1,256,1024]{2,1,0:T(8,128)(2,1)S(1)}, u32[]{:S(2)}, u32[]{:S(2)}) collective-permute-start(bf16[1,256,1024]{2,1,0:T(8,128)(2,1)} %param.10), channel_id=1, source_target_pairs={{0,4},{6,2},{1,5},{7,3},{8,12},{14,10},{9,13},{15,11},{16,20},{22,... | collective-permute-start | bytes 1572872 | tf_op jit(solution)/shard_map/ppermute | solution.py:255
  6.0 15.1 %collective-permute-start.3 = (bf16[1,256,1024]{2,1,0:T(8,128)(2,1)}, bf16[1,256,1024]{2,1,0:T(8,128)(2,1)S(1)}, u32[]{:S(2)}, u32[]{:S(2)}) collective-permute-start(bf16[1,256,1024]{2,1,0:T(8,128)(2,1)} %param.11), channel_id=1, source_target_pairs={{0,8},{8,0},{16,24},{24,16},{1,9},{9,1},{17,25},{25,17},{2,10},{10... | collective-permute-start | bytes 1572872 | tf_op jit(solution)/shard_map/ppermute | solution.py:228
  7.6 24.5 %collective-permute-start.4 = (bf16[1,256,1024]{2,1,0:T(8,128)(2,1)}, bf16[1,256,1024]{2,1,0:T(8,128)(2,1)S(1)}, u32[]{:S(2)}, u32[]{:S(2)}) collective-permute-start(bf16[1,256,1024]{2,1,0:T(8,128)(2,1)} %param.11), channel_id=1, source_target_pairs={{0,16},{8,24},{16,0},{24,8},{1,17},{9,25},{17,1},{25,9},{2,18},{10... | collective-permute-start | bytes 1572872 | tf_op jit(solution)/shard_map/ppermute | solution.py:228
  9.1 36.4 %collective-permute-start = (bf16[1,256,1024]{2,1,0:T(8,128)(2,1)}, bf16[1,256,1024]{2,1,0:T(8,128)(2,1)S(1)}, u32[]{:S(2)}, u32[]{:S(2)}) collective-permute-start(bf16[1,256,1024]{2,1,0:T(8,128)(2,1)} %param.10), channel_id=1, source_target_pairs={{2,4},{4,2},{3,5},{5,3},{10,12},{12,10},{11,13},{13,11},{18,20},{2... | collective-permute-start | bytes 1572872 | tf_op jit(solution)/shard_map/ppermute | solution.py:258
  9.8 32.3 %collective-permute-start.5 = (bf16[1,256,1024]{2,1,0:T(8,128)(2,1)}, bf16[1,256,1024]{2,1,0:T(8,128)(2,1)S(1)}, u32[]{:S(2)}, u32[]{:S(2)}) collective-permute-start(bf16[1,256,1024]{2,1,0:T(8,128)(2,1)} %param.11), channel_id=1, source_target_pairs={{0,24},{8,16},{16,8},{24,0},{1,25},{9,17},{17,9},{25,1},{2,26},{10... | collective-permute-start | bytes 1572872 | tf_op jit(solution)/shard_map/ppermute | solution.py:228
  10.4 0.7 copy-start.2
  11.0 0.7 copy-start.3
  11.7 6.2 %copy-start.1 = (bf16[1,256,1024]{2,1,0:T(8,128)(2,1)S(1)}, bf16[1,256,1024]{2,1,0:T(8,128)(2,1)}, u32[]{:S(2)}) copy-start(bf16[1,256,1024]{2,1,0:T(8,128)(2,1)} %param.10) | copy-start | bytes 1572868
  17.9 26.1 %collective-permute-start.6 = (bf16[1,256,1024]{2,1,0:T(8,128)(2,1)S(1)}, bf16[1,256,1024]{2,1,0:T(8,128)(2,1)S(1)}, u32[]{:S(2)}, u32[]{:S(2)}) collective-permute-start(bf16[1,256,1024]{2,1,0:T(8,128)(2,1)S(1)} %copy-done.1), channel_id=1, source_target_pairs={{0,2},{2,0},{4,6},{6,4},{1,3},{3,1},{5,7},{7,5},{8,10},{10,8},{12,... | collective-permute-start | bytes 1572872 | tf_op jit(solution)/shard_map/ppermute | solution.py:257
  21.1 23.0 %collective-permute-start.7 = (bf16[1,256,1024]{2,1,0:T(8,128)(2,1)S(1)}, bf16[1,256,1024]{2,1,0:T(8,128)(2,1)S(1)}, u32[]{:S(2)}, u32[]{:S(2)}) collective-permute-start(bf16[1,256,1024]{2,1,0:T(8,128)(2,1)S(1)} %copy-done.1), channel_id=1, source_target_pairs={{2,6},{4,0},{3,7},{5,1},{10,14},{12,8},{11,15},{13,9},{18,22},{20,... | collective-permute-start | bytes 1572872 | tf_op jit(solution)/shard_map/ppermute | solution.py:256
  32.1 21.2 %collective-permute-start.2 = (bf16[1,256,1024]{2,1,0:T(8,128)(2,1)S(1)}, bf16[1,256,1024]{2,1,0:T(8,128)(2,1)S(1)}, u32[]{:S(2)}, u32[]{:S(2)}) collective-permute-start(bf16[1,256,1024]{2,1,0:T(8,128)(2,1)S(1)} %collective-permute-done.1), channel_id=1, source_target_pairs={{4,6},{2,0},{5,7},{3,1},{12,14},{10,8},{13,15},{11,9},{20,22},{18,... | collective-permute-start | bytes 1572872 | tf_op jit(solution)/shard_map/ppermute | solution.py:259
  33.4 4.8 %copy-start = (bf16[1,256,1024]{2,1,0:T(8,128)(2,1)S(1)}, bf16[1,256,1024]{2,1,0:T(8,128)(2,1)}, u32[]{:S(2)}) copy-start(bf16[1,256,1024]{2,1,0:T(8,128)(2,1)} %param.11) | copy-start | bytes 1572868

commit v4 on v3

--- a/solution.py
+++ b/solution.py
@@ -34,11 +34,12 @@
     ).astype(jnp.bfloat16)
 
 
-def shifts(arrivals, nband, bpiece, places, place_ref, index_ref, energy_ref):
+def shifts(arrivals, nband, bpiece, places, index_ref, energy_ref):
+    row, group = lax.axis_index("row"), lax.axis_index("band")
     out = []
     for n in places:
         for k in range(bpiece):
-            band = (arrivals(n, place_ref[0]) * nband + place_ref[2]) * bpiece + k
+            band = (arrivals(n, row) * nband + group) * bpiece + k
             for w in range(index_ref.shape[0]):
                 out.append(-4.0 + 0.25 * index_ref[w].astype(jnp.float32) - energy_ref[band])
     return out
@@ -48,7 +49,6 @@
     arrivals,
     nband,
     bpiece,
-    place_ref,
     index_ref,
     energy_ref,
     amp_hbm,
@@ -71,7 +71,7 @@
     for i in range(steps):
         for copy in copies(i):
             copy.start()
-    xs = shifts(arrivals, nband, bpiece, (0, 1), place_ref, index_ref, energy_ref)
+    xs = shifts(arrivals, nband, bpiece, (0, 1), index_ref, energy_ref)
 
     @pl.loop(0, steps)
     def _(i):
@@ -84,14 +84,14 @@
             store_screened(xs, amp_ref, freq_ref, here, COLUMNS, ahead_ref)
 
 
-def screen(place, arrivals, nband, bpiece, freq_index, band_energy, amp, freq):
+def screen(arrivals, nband, bpiece, freq_index, band_energy, amp, freq):
     g, h = amp.shape
     nfreq = freq_index.shape[0]
     rows = min(ROWS, g)
     held = 8 * g * h + 4 * nfreq * g * bpiece * h
     return pl.pallas_call(
         functools.partial(screen_kernel, arrivals, nband, bpiece),
-        in_specs=[SCALARS] * 3 + [pl.BlockSpec(memory_space=pl.ANY)] * 2,
+        in_specs=[SCALARS] * 2 + [pl.BlockSpec(memory_space=pl.ANY)] * 2,
         out_specs=[WHOLE] * 3,
         out_shape=[
             jax.ShapeDtypeStruct((2 * bpiece, nfreq, g, h), jnp.bfloat16),
@@ -105,7 +105,6 @@
         compiler_params=pltpu.CompilerParams(vmem_limit_bytes=VMEM_LIMIT + held),
         name="screen",
     )(
-        place,
         freq_index,
         band_energy,
         *(pltpu.with_memory_space_constraint(x, pltpu.HBM) for x in (amp, freq)),
@@ -113,10 +112,10 @@
 
 
 def more_kernel(
-    arrivals, nband, bpiece, place_ref, index_ref, energy_ref, amp_ref, freq_ref, ahead_ref
+    arrivals, nband, bpiece, index_ref, energy_ref, amp_ref, freq_ref, ahead_ref
 ):
     places = range(2, 2 + ahead_ref.shape[0] // bpiece)
-    xs = shifts(arrivals, nband, bpiece, places, place_ref, index_ref, energy_ref)
+    xs = shifts(arrivals, nband, bpiece, places, index_ref, energy_ref)
 
     @pl.loop(0, amp_ref.shape[0] // SMALL)
     def _(i):
@@ -124,13 +123,13 @@
         store_screened(xs, amp_ref, freq_ref, here, COLUMNS, ahead_ref)
 
 
-def screen_more(place, arrivals, nband, count, bpiece, freq_index, band_energy, amp, freq):
+def screen_more(arrivals, nband, count, bpiece, freq_index, band_energy, amp, freq):
     g, h = amp.shape
     nfreq = freq_index.shape[0]
     held = 8 * g * h + 2 * nfreq * g * h * count * bpiece
     return pl.pallas_call(
         functools.partial(more_kernel, arrivals, nband, bpiece),
-        in_specs=[SCALARS] * 3 + [WHOLE] * 2,
+        in_specs=[SCALARS] * 2 + [WHOLE] * 2,
         out_specs=WHOLE,
         out_shape=jax.ShapeDtypeStruct((count * bpiece, nfreq, g, h), jnp.bfloat16),
         cost_estimate=pl.CostEstimate(
@@ -138,7 +137,7 @@
         ),
         compiler_params=pltpu.CompilerParams(vmem_limit_bytes=VMEM_LIMIT + held),
         name="more",
-    )(place, freq_index, band_energy, amp, freq)
+    )(freq_index, band_energy, amp, freq)
 
 
 def apply_kernel(first, ahead_ref, *refs):
@@ -239,7 +238,6 @@
     nband, nrow, ncol = (lax.axis_size(a) for a in ("band", "row", "col"))
     axes = ("row", "col", "band")
     line = is_line(ncol)
-    place = jnp.stack([lax.axis_index(a) for a in axes]).astype(jnp.int32)
 
     rights, whose = gather_xor(right_pieces, "row")
     if nrow & (nrow - 1):
@@ -275,8 +273,8 @@
         ]
 
     scalars = freq_index, band_energy
-    ahead, amp, freq = screen(place, whose, nband, bpiece, *scalars, pole_amp, pole_freq)
-    later = screen_more(place, whose, nband, nrow - 2, bpiece, *scalars, amp, freq)
+    ahead, amp, freq = screen(whose, nband, bpiece, *scalars, pole_amp, pole_freq)
+    later = screen_more(whose, nband, nrow - 2, bpiece, *scalars, amp, freq)
     tables = []
     for d in range(nrow):
         source, first = (ahead, d) if d < 2 else (later, d - 2)

time: 69.5 us -> 69.6 us (level)
  no operation moved by 1% of the time
where the time goes in v4:
time: 69.6 us; the launch traced here: 69.1 us
  waiting for transfers between devices  19.5 us (28%)
  Pallas kernels  18 us (26%)
  starting transfers between devices  14.9 us (21%)
  blocking collectives  14.5 us (21%)
  local copies, waits for them, and re-layouts  1.32 us (2%)
    all_to_all x1, blocking collectives, body(): parts = lax.all_to_all(total, axes, split_axis=0, concat_axis=0, tiled=True)  14.5 us
    ppermute x3, waiting for transfers between devices, gather_xor(): lax.ppermute(piece, axis, xor_pairs(n, d))  11 us
    ppermute x1, waiting for transfers between devices, body(): hop = lax.ppermute(inward, 'col', [(2, 3), (1, 0)])  7.91 us
    pallas_call x1, Pallas kernels, screen(): pl.pallas_call(functools.partial(screen_kernel, arrivals, nband, bpiece),...  6.2 us
    ppermute x1, starting transfers between devices, body(): inward = lax.ppermute(left_pieces, 'col', [(0, 2), (3, 1)])  6.12 us
    pallas_call x4, Pallas kernels, apply_rights(): pl.pallas_call(functools.partial(apply_kernel, first), in_specs=[WHOLE] *...  5.12 us
    pallas_call x1, Pallas kernels, screen_more(): pl.pallas_call(functools.partial(more_kernel, arrivals, nband, bpiece), i...  4.77 us
    ppermute x3, starting transfers between devices, gather_xor(): lax.ppermute(piece, axis, xor_pairs(n, d))  3.62 us
  transfers between devices with their start and end apart: 8, of which 4 were waited for; matrix products, arithmetic and copies ran while one was open for 0% of the time, Pallas kernels for 25%

profile of v4, /device:TPU:0, one launch (start us, length us, event | category | flops | bytes accessed | tf_op | source)
XLA Modules:
  0.0 69.1 jit_solution(8275437694374506997)
XLA Ops:
  0.0 0.0 copy-start.1
  0.0 6.1 %collective-permute-start.1 = (bf16[1,256,1024]{2,1,0:T(8,128)(2,1)}, bf16[1,256,1024]{2,1,0:T(8,128)(2,1)S(1)}, u32[]{:S(2)}, u32[]{:S(2)}) collective-permute-start(bf16[1,256,1024]{2,1,0:T(8,128)(2,1)} %param.10), channel_id=1, source_target_pairs={{0,4},{6,2},{1,5},{7,3},{8,12},{14,10},{9,13},{15,11},{16,20},{22,... | collective-permute-start | bytes 1572872 | tf_op jit(solution)/shard_map/ppermute | solution.py:253
  6.1 1.6 %collective-permute-start.3 = (bf16[1,256,1024]{2,1,0:T(8,128)(2,1)}, bf16[1,256,1024]{2,1,0:T(8,128)(2,1)S(1)}, u32[]{:S(2)}, u32[]{:S(2)}) collective-permute-start(bf16[1,256,1024]{2,1,0:T(8,128)(2,1)} %param.11), channel_id=1, source_target_pairs={{0,8},{8,0},{16,24},{24,16},{1,9},{9,1},{17,25},{25,17},{2,10},{10... | collective-permute-start | bytes 1572872 | tf_op jit(solution)/shard_map/ppermute | solution.py:227
  7.7 1.5 %collective-permute-start.4 = (bf16[1,256,1024]{2,1,0:T(8,128)(2,1)}, bf16[1,256,1024]{2,1,0:T(8,128)(2,1)S(1)}, u32[]{:S(2)}, u32[]{:S(2)}) collective-permute-start(bf16[1,256,1024]{2,1,0:T(8,128)(2,1)} %param.11), channel_id=1, source_target_pairs={{0,16},{8,24},{16,0},{24,8},{1,17},{9,25},{17,1},{25,9},{2,18},{10... | collective-permute-start | bytes 1572872 | tf_op jit(solution)/shard_map/ppermute | solution.py:227
  9.2 0.7 collective-permute-start
  9.9 0.5 collective-permute-start.5
  10.4 0.7 copy-done.2
  11.1 0.7 copy-done.3
  11.8 6.2 %screen.1 = (bf16[2,2,1024,1024]{3,2,1,0:T(8,128)(2,1)S(1)}, f32[1024,1024]{1,0:T(8,128)S(1)}, f32[1024,1024]{1,0:T(8,128)S(1)}) custom-call(s32[2]{0:T(128)S(1)} %copy-done.2, f32[8]{0:T(128)S(1)} %copy-done.3, f32[1024,1024]{1,0:T(8,128)} %amp_hbm.1, f32[1024,1024]{1,0:T(8,128)} %freq_hbm.1), custom_call_target="tpu_custom_call" | custom-call | flops 2147483648 | bytes 8388608 | tf_op jit(solution)/shard_map/screen/pallas_call | solution.py:92
  18.0 0.0 collective-permute-done.1
  18.0 0.0 copy-done.1
  18.0 2.0 %collective-permute-start.6 = (bf16[1,256,1024]{2,1,0:T(8,128)(2,1)S(1)}, bf16[1,256,1024]{2,1,0:T(8,128)(2,1)S(1)}, u32[]{:S(2)}, u32[]{:S(2)}) collective-permute-start(bf16[1,256,1024]{2,1,0:T(8,128)(2,1)S(1)} %copy-done.1), channel_id=1, source_target_pairs={{0,2},{2,0},{4,6},{6,4},{1,3},{3,1},{5,7},{7,5},{8,10},{10,8},{12,... | collective-permute-start | bytes 1572872 | tf_op jit(solution)/shard_map/ppermute | solution.py:255
  19.9 1.3 %collective-permute-done.3 = bf16[1,256,1024]{2,1,0:T(8,128)(2,1)S(1)} collective-permute-done((bf16[1,256,1024]{2,1,0:T(8,128)(2,1)}, bf16[1,256,1024]{2,1,0:T(8,128)(2,1)S(1)}, u32[]{:S(2)}, u32[]{:S(2)}) %collective-permute-start.3) | collective-permute-done | bytes 524320 | tf_op jit(solution)/shard_map/ppermute | solution.py:227
  21.2 1.3 %collective-permute-start.7 = (bf16[1,256,1024]{2,1,0:T(8,128)(2,1)S(1)}, bf16[1,256,1024]{2,1,0:T(8,128)(2,1)S(1)}, u32[]{:S(2)}, u32[]{:S(2)}) collective-permute-start(bf16[1,256,1024]{2,1,0:T(8,128)(2,1)S(1)} %copy-done.1), channel_id=1, source_target_pairs={{2,6},{4,0},{3,7},{5,1},{10,14},{12,8},{11,15},{13,9},{18,22},{20,... | collective-permute-start | bytes 1572872 | tf_op jit(solution)/shard_map/ppermute | solution.py:254
  22.5 9.7 %collective-permute-done.4 = bf16[1,256,1024]{2,1,0:T(8,128)(2,1)S(1)} collective-permute-done((bf16[1,256,1024]{2,1,0:T(8,128)(2,1)}, bf16[1,256,1024]{2,1,0:T(8,128)(2,1)S(1)}, u32[]{:S(2)}, u32[]{:S(2)}) %collective-permute-start.4) | collective-permute-done | bytes 524320 | tf_op jit(solution)/shard_map/ppermute | solution.py:227
  32.2 1.3 %collective-permute-start.2 = (bf16[1,256,1024]{2,1,0:T(8,128)(2,1)S(1)}, bf16[1,256,1024]{2,1,0:T(8,128)(2,1)S(1)}, u32[]{:S(2)}, u32[]{:S(2)}) collective-permute-start(bf16[1,256,1024]{2,1,0:T(8,128)(2,1)S(1)} %collective-permute-done.1), channel_id=1, source_target_pairs={{4,6},{2,0},{5,7},{3,1},{12,14},{10,8},{13,15},{11,9},{20,22},{18,... | collective-permute-start | bytes 1572872 | tf_op jit(solution)/shard_map/ppermute | solution.py:257
  33.5 0.0 copy-start
  33.5 4.8 %more.1.ahead_ref = bf16[2,2,1024,1024]{3,2,1,0:T(8,128)(2,1)S(1)} custom-call(s32[2]{0:T(128)S(1)} %copy-done.2, f32[8]{0:T(128)S(1)} %copy-done.3, f32[1024,1024]{1,0:T(8,128)S(1)} %get-tuple-element.9.amp_ref, f32[1024,1024]{1,0:T(8,128)S(1)} %get-tuple-element.10.freq_ref), custom_call_target="tpu_custom_call" | custom-call | flops 2147483648 | bytes 8388608 | tf_op jit(solution)/shard_map/more/pallas_call | solution.py:130
  38.3 0.0 copy-done
  38.3 1.3 %apply.4.rest_4_.rest_2_ = bf16[1,1024,512]{2,1,0:T(8,128)(2,1)S(1)} custom-call(bf16[2,2,1024,1024]{3,2,1,0:T(8,128)(2,1)S(1)} %get-tuple-element.8.ahead_ref, bf16[256,1024]{1,0:T(8,128)(2,1)S(1)} %bitcast.15), custom_call_target="tpu_custom_call" | custom-call | flops 1073741824 | bytes 4194304 | tf_op jit(solution)/shard_map/apply/pallas_call | solution.py:157
  39.6 1.3 %apply.5.rest_5_.rest_3_ = bf16[1,1024,512]{2,1,0:T(8,128)(2,1)S(1)} custom-call(bf16[2,2,1024,1024]{3,2,1,0:T(8,128)(2,1)S(1)} %get-tuple-element.8.ahead_ref, bf16[256,1024]{1,0:T(8,128)(2,1)S(1)} %bitcast.17), custom_call_target="tpu_custom_call" | custom-call | flops 1073741824 | bytes 4194304 | tf_op jit(solution)/shard_map/apply/pallas_call | solution.py:157
  40.9 1.3 %apply.6.rest_6_.rest_4_ = bf16[1,1024,512]{2,1,0:T(8,128)(2,1)S(1)} custom-call(bf16[2,2,1024,1024]{3,2,1,0:T(8,128)(2,1)S(1)} %more.1.ahead_ref, bf16[256,1024]{1,0:T(8,128)(2,1)S(1)} %bitcast.18), custom_call_target="tpu_custom_call" | custom-call | flops 1073741824 | bytes 4194304 | tf_op jit(solution)/shard_map/apply/pallas_call | solution.py:157
  42.2 0.0 collective-permute-done.5
  42.2 1.3 %apply.7.rest_7_.rest_5_ = bf16[1,1024,512]{2,1,0:T(8,128)(2,1)S(1)} custom-call(bf16[2,2,1024,1024]{3,2,1,0:T(8,128)(2,1)S(1)} %more.1.ahead_ref, bf16[256,1024]{1,0:T(8,128)(2,1)S(1)} %bitcast.19), custom_call_target="tpu_custom_call" | custom-call | flops 1073741824 | bytes 4194304 | tf_op jit(solution)/shard_map/apply/pallas_call | solution.py:157
  43.5 0.6 collective-permute-done.6
  44.1 0.0 collective-permute-done.7
  44.1 1.4 %fold.2.rest_6_ = f32[256,512]{1,0:T(8,128)S(1)} custom-call(bf16[256,1024]{1,0:T(8,128)(2,1)S(1)} %bitcast.21, bf16[256,1024]{1,0:T(8,128)(2,1)S(1)} %bitcast.23, bf16[256,1024]{1,0:T(8,128)(2,1)S(1)} %bitcast.22, bf16[256,1024]{1,0:T(8,128)(2,1)S(1)} %bitcast.24, bf16[1,1024,512]{2,1,0:T(8,128)(2,1)S(1)} %apply.4.rest_4_.rest_2_, ...), custom_call_target="tpu_custom_call" | custom-call | flops 1073741824 | bytes 6291456 | tf_op jit(solution)/shard_map/fold/pallas_call | solution.py:199
  45.5 0.0 collective-permute-done
  45.5 7.9 %collective-permute-done.2 = bf16[1,256,1024]{2,1,0:T(8,128)(2,1)S(1)} collective-permute-done((bf16[1,256,1024]{2,1,0:T(8,128)(2,1)S(1)}, bf16[1,256,1024]{2,1,0:T(8,128)(2,1)S(1)}, u32[]{:S(2)}, u32[]{:S(2)}) %collective-permute-start.2) | collective-permute-done | bytes 524320 | tf_op jit(solution)/shard_map/ppermute | solution.py:257
  53.4 0.5 fold.3
  54.0 14.5 %all_to_all.9 = bf16[32,8,512]{2,1,0:T(8,128)(2,1)S(1)} all-to-all(bf16[32,8,512]{2,1,0:T(8,128)(2,1)S(1)} %bitcast.14), channel_id=1, replica_groups=mesh['row'=4,'col'=4,'band'=2] {'row','col','band'}, dimensions={0} | all-to-all | bytes 524288 | tf_op jit(solution)/shard_map/all_to_all | solution.py:288
  68.5 0.7 convert_reduce_fusion
  (2 shorter events, 0.0 us)
Async XLA Ops:
  0.0 18.0 %copy-start.1 = (bf16[1,256,1024]{2,1,0:T(8,128)(2,1)S(1)}, bf16[1,256,1024]{2,1,0:T(8,128)(2,1)}, u32[]{:S(2)}) copy-start(bf16[1,256,1024]{2,1,0:T(8,128)(2,1)} %param.10) | copy-start | bytes 1572868
  0.0 18.0 %collective-permute-start.1 = (bf16[1,256,1024]{2,1,0:T(8,128)(2,1)}, bf16[1,256,1024]{2,1,0:T(8,128)(2,1)S(1)}, u32[]{:S(2)}, u32[]{:S(2)}) collective-permute-start(bf16[1,256,1024]{2,1,0:T(8,128)(2,1)} %param.10), channel_id=1, source_target_pairs={{0,4},{6,2},{1,5},{7,3},{8,12},{14,10},{9,13},{15,11},{16,20},{22,... | collective-permute-start | bytes 1572872 | tf_op jit(solution)/shard_map/ppermute | solution.py:253
  6.1 15.1 %collective-permute-start.3 = (bf16[1,256,1024]{2,1,0:T(8,128)(2,1)}, bf16[1,256,1024]{2,1,0:T(8,128)(2,1)S(1)}, u32[]{:S(2)}, u32[]{:S(2)}) collective-permute-start(bf16[1,256,1024]{2,1,0:T(8,128)(2,1)} %param.11), channel_id=1, source_target_pairs={{0,8},{8,0},{16,24},{24,16},{1,9},{9,1},{17,25},{25,17},{2,10},{10... | collective-permute-start | bytes 1572872 | tf_op jit(solution)/shard_map/ppermute | solution.py:227
  7.7 24.5 %collective-permute-start.4 = (bf16[1,256,1024]{2,1,0:T(8,128)(2,1)}, bf16[1,256,1024]{2,1,0:T(8,128)(2,1)S(1)}, u32[]{:S(2)}, u32[]{:S(2)}) collective-permute-start(bf16[1,256,1024]{2,1,0:T(8,128)(2,1)} %param.11), channel_id=1, source_target_pairs={{0,16},{8,24},{16,0},{24,8},{1,17},{9,25},{17,1},{25,9},{2,18},{10... | collective-permute-start | bytes 1572872 | tf_op jit(solution)/shard_map/ppermute | solution.py:227
  9.2 36.3 %collective-permute-start = (bf16[1,256,1024]{2,1,0:T(8,128)(2,1)}, bf16[1,256,1024]{2,1,0:T(8,128)(2,1)S(1)}, u32[]{:S(2)}, u32[]{:S(2)}) collective-permute-start(bf16[1,256,1024]{2,1,0:T(8,128)(2,1)} %param.10), channel_id=1, source_target_pairs={{2,4},{4,2},{3,5},{5,3},{10,12},{12,10},{11,13},{13,11},{18,20},{2... | collective-permute-start | bytes 1572872 | tf_op jit(solution)/shard_map/ppermute | solution.py:256
  9.9 32.3 %collective-permute-start.5 = (bf16[1,256,1024]{2,1,0:T(8,128)(2,1)}, bf16[1,256,1024]{2,1,0:T(8,128)(2,1)S(1)}, u32[]{:S(2)}, u32[]{:S(2)}) collective-permute-start(bf16[1,256,1024]{2,1,0:T(8,128)(2,1)} %param.11), channel_id=1, source_target_pairs={{0,24},{8,16},{16,8},{24,0},{1,25},{9,17},{17,9},{25,1},{2,26},{10... | collective-permute-start | bytes 1572872 | tf_op jit(solution)/shard_map/ppermute | solution.py:227
  10.4 0.7 copy-start.2
  11.1 0.7 copy-start.3
  18.0 26.1 %collective-permute-start.6 = (bf16[1,256,1024]{2,1,0:T(8,128)(2,1)S(1)}, bf16[1,256,1024]{2,1,0:T(8,128)(2,1)S(1)}, u32[]{:S(2)}, u32[]{:S(2)}) collective-permute-start(bf16[1,256,1024]{2,1,0:T(8,128)(2,1)S(1)} %copy-done.1), channel_id=1, source_target_pairs={{0,2},{2,0},{4,6},{6,4},{1,3},{3,1},{5,7},{7,5},{8,10},{10,8},{12,... | collective-permute-start | bytes 1572872 | tf_op jit(solution)/shard_map/ppermute | solution.py:255
  21.2 22.9 %collective-permute-start.7 = (bf16[1,256,1024]{2,1,0:T(8,128)(2,1)S(1)}, bf16[1,256,1024]{2,1,0:T(8,128)(2,1)S(1)}, u32[]{:S(2)}, u32[]{:S(2)}) collective-permute-start(bf16[1,256,1024]{2,1,0:T(8,128)(2,1)S(1)} %copy-done.1), channel_id=1, source_target_pairs={{2,6},{4,0},{3,7},{5,1},{10,14},{12,8},{11,15},{13,9},{18,22},{20,... | collective-permute-start | bytes 1572872 | tf_op jit(solution)/shard_map/ppermute | solution.py:254
  32.2 21.2 %collective-permute-start.2 = (bf16[1,256,1024]{2,1,0:T(8,128)(2,1)S(1)}, bf16[1,256,1024]{2,1,0:T(8,128)(2,1)S(1)}, u32[]{:S(2)}, u32[]{:S(2)}) collective-permute-start(bf16[1,256,1024]{2,1,0:T(8,128)(2,1)S(1)} %collective-permute-done.1), channel_id=1, source_target_pairs={{4,6},{2,0},{5,7},{3,1},{12,14},{10,8},{13,15},{11,9},{20,22},{18,... | collective-permute-start | bytes 1572872 | tf_op jit(solution)/shard_map/ppermute | solution.py:257
  33.5 4.8 %copy-start = (bf16[1,256,1024]{2,1,0:T(8,128)(2,1)S(1)}, bf16[1,256,1024]{2,1,0:T(8,128)(2,1)}, u32[]{:S(2)}) copy-start(bf16[1,256,1024]{2,1,0:T(8,128)(2,1)} %param.11) | copy-start | bytes 1572868
